TPU v7x, 256 devices: a whole 4x4x8 slice. The times are simulated.
256 devices in a mesh: ga: 8 (over z_lo, core), band: 32 (over x, z_hi, y).
Axes of the slice: x: 4, y: 4, z: 8 (z_hi: 2, z_lo: 4; z = z_hi * 4 + z_lo), core: 2. Of those that a mesh axis runs over, the one named last changes fastest.
Arguments:
- orbitals: bfloat16 [1024, 2, 65536], P('band', None, 'ga'), may hold values from -6 to 6
- projectors: bfloat16 [864, 2, 65536], P(None, None, ('ga', 'band')), may hold values from -0.015625 to 0.015625
- coupling: float32 [4, 18, 18], replicated, may hold values from -12 to 12
- species: int32 [48], replicated, may hold values from 0 to 3
- offsets: int32 [48], replicated, may hold values from 0 to 846, as said below
Outputs:
- applied: bfloat16 [1024, 2, 65536], P('band', None, 'ga')
Inputs may be any that keep to these rules, and one draw needn't show every extreme that they name: Each atom's 18 projectors are the 18 consecutive rows of projectors starting at its offset; offsets are multiples of 18, and the atoms' blocks are distinct and cover all 864 rows.
All inputs are finite; a program needn't handle non-finite values.
Results may differ from a plain program's by a relative error of at most 0.0049.
Values may be sent and summed in bfloat16 or wider, within the bound.
A program may use at most 64 MiB of HBM per device.

v0:
```python
import jax
import jax.numpy as jnp
from jax import lax
from jax.sharding import PartitionSpec as P


def swapped(array, axis, apart):
    return lax.ppermute(array, axis, [(i, i ^ 1 << apart) for i in range(lax.axis_size(axis))])


def block_matrices(coupling, species, offsets):
    per_atom = coupling.shape[1]
    count = offsets.shape[0]
    blocks = jnp.arange(count, dtype=jnp.int32)
    matches = (offsets[None, :] == blocks[:, None] * per_atom).astype(jnp.int32)
    atom_kind = jnp.sum(matches * species[None, :], axis=1)
    onehot = (atom_kind[:, None] == jnp.arange(coupling.shape[0], dtype=jnp.int32)[None, :]).astype(
        jnp.float32
    )
    table = coupling.reshape(coupling.shape[0], per_atom * per_atom)
    picked = jnp.dot(
        onehot, table, precision=lax.Precision.HIGHEST, preferred_element_type=jnp.float32
    )
    return picked.reshape(count, per_atom, per_atom)


def apply_coupling(matrices, becp):
    count = matrices.shape[0]
    per_atom = matrices.shape[1]
    height = becp.shape[0]
    widths = becp.shape[2]
    blocked = becp.reshape(count, per_atom, 2 * widths)
    coupled = jnp.einsum("aij,ajc->aic", matrices, blocked, precision=lax.Precision.HIGHEST)
    return coupled.reshape(height, 2, widths).astype(jnp.bfloat16)


def project_bands(projectors, spread):
    total_proj = projectors.shape[0]
    total_bands = spread.shape[0]
    flat_proj = projectors.reshape(total_proj, -1)
    turned = jnp.concatenate([spread[:, 1, :], -spread[:, 0, :]], axis=1)
    stacked = jnp.concatenate([spread.reshape(total_bands, -1), turned], axis=0)
    partial_value = lax.dot_general(
        flat_proj, stacked, (((1,), (1,)), ((), ())), preferred_element_type=jnp.float32
    )
    return partial_value.reshape(total_proj, 2, total_bands)


def add_back(projectors, dbecp):
    total_proj = projectors.shape[0]
    total_bands = dbecp.shape[2]
    columns = dbecp.reshape(total_proj, 2 * total_bands)
    real_part = lax.dot_general(
        columns, projectors[:, 0, :], (((0,), (0,)), ((), ())), preferred_element_type=jnp.float32
    )
    imag_part = lax.dot_general(
        columns, projectors[:, 1, :], (((0,), (0,)), ((), ())), preferred_element_type=jnp.float32
    )
    out_real = real_part[:total_bands] - imag_part[total_bands:]
    out_imag = imag_part[:total_bands] + real_part[total_bands:]
    return jnp.stack([out_real, out_imag], axis=1).astype(jnp.bfloat16)


def grid_apply(orbitals, projectors, matrices):
    parts = lax.axis_size("band")
    levels = parts.bit_length() - 1
    low_bits = levels - 2
    groups = 2**low_bits
    place = lax.axis_index("band")
    width = projectors.shape[2]
    bands_here = orbitals.shape[0]
    current = orbitals.reshape(bands_here, 2, 4, groups, width)
    for bit in range(low_bits - 1, -1, -1):
        flag = place // 2**bit % 2
        half = current.shape[3] // 2
        lower = current[:, :, :, :half]
        upper = current[:, :, :, half:]
        keep = jnp.where(flag == 0, lower, upper)
        send = jnp.where(flag == 0, upper, lower)
        got = swapped(send, "band", bit)
        current = jnp.where(
            flag == 0, jnp.concatenate([keep, got], 0), jnp.concatenate([got, keep], 0)
        )
    spread = current.reshape(current.shape[0], 2, 4 * width)
    gathered = projectors
    for bit in range(low_bits, levels):
        flag = place // 2**bit % 2
        got = swapped(gathered, "band", bit)
        gathered = jnp.where(
            flag == 0, jnp.concatenate([gathered, got], 2), jnp.concatenate([got, gathered], 2)
        )
    partial_value = project_bands(gathered, spread)
    becp = lax.psum(partial_value, "ga")
    for bit in range(low_bits):
        becp = becp + swapped(becp, "band", bit)
    dbecp = apply_coupling(matrices, becp)
    result = add_back(gathered, dbecp)
    result = result.reshape(result.shape[0], 2, 4, 1, width)
    for bit in range(low_bits):
        flag = place // 2**bit % 2
        half = result.shape[0] // 2
        lower = result[:half]
        upper = result[half:]
        keep = jnp.where(flag == 0, lower, upper)
        send = jnp.where(flag == 0, upper, lower)
        got = swapped(send, "band", bit)
        result = jnp.where(
            flag == 0, jnp.concatenate([keep, got], 3), jnp.concatenate([got, keep], 3)
        )
    return result.reshape(bands_here, 2, 4 * groups * width)


def per_device(orbitals, projectors, coupling, species, offsets):
    matrices = block_matrices(coupling, species, offsets)
    return grid_apply(orbitals, projectors, matrices)


def solution(mesh):
    placed = (P("band", None, "ga"), P(None, None, ("ga", "band")), P(), P(), P())
    return jax.shard_map(
        per_device, mesh=mesh, in_specs=placed, out_specs=P("band", None, "ga"), check_vma=False
    )
```

profile of v0, /device:TPU:32, one launch (start us, length us, event | category | flops | bytes accessed | tf_op | source)
XLA Modules:
  0.0 412.8 jit_solution(13116322891664677685)
XLA Ops:
  6.5 1.7 reshape.119
  8.3 0.6 fusion.13
  8.9 0.5 broadcast_select_fusion.11
  9.4 6.4 %collective-permute-start.2 = (bf16[32,2,4,4,256]{4,2,0,1,3:T(4,128)(2,1)S(1)}, bf16[32,2,4,4,256]{4,2,0,1,3:T(4,128)(2,1)S(1)}, u32[]{:S(2)}, u32[]{:S(2)}) collective-permute-start(bf16[32,2,4,4,256]{4,2,0,1,3:T(4,128)(2,1)S(1)} %get-tuple-element.20), channel_id=1, source_target_pairs={{0,4},{1,5},{2,6},{3,7},{4,0},{5,1},{6,2},{7,3},{8,12},{9,13},{10,... | collective-permute-start | bytes 1572872 | tf_op jit(solution)/shard_map/ppermute | solution.py:8
  15.9 1.6 collective-permute-start
  17.5 21.6 %collective-permute-done.2 = bf16[32,2,4,4,256]{4,2,0,1,3:T(4,128)(2,1)S(1)} collective-permute-done((bf16[32,2,4,4,256]{4,2,0,1,3:T(4,128)(2,1)S(1)}, bf16[32,2,4,4,256]{4,2,0,1,3:T(4,128)(2,1)S(1)}, u32[]{:S(2)}, u32[]{:S(2)}) %collective-permute-start.2) | collective-permute-done | bytes 524320 | tf_op jit(solution)/shard_map/ppermute | solution.py:8
  39.1 1.2 maximum_select_fusion.2
  40.2 1.2 broadcast_select_fusion.7
  41.5 3.2 collective-permute-start.3
  44.7 1.9 maximum_select_fusion.1
  46.6 3.1 collective-permute-start.1
  49.7 6.6 %collective-permute-done.3 = bf16[64,2,4,2,256]{4,2,0,1,3:T(4,128)(2,1)} collective-permute-done((bf16[64,2,4,2,256]{4,2,0,1,3:T(4,128)(2,1)}, bf16[64,2,4,2,256]{4,2,0,1,3:T(4,128)(2,1)}, u32[]{:S(2)}, u32[]{:S(2)}) %collective-permute-start.3) | collective-permute-done | bytes 524320 | tf_op jit(solution)/shard_map/ppermute | solution.py:8
  56.2 2.4 maximum_select_fusion.3
  58.6 1.2 broadcast_select_fusion.1
  59.9 1.6 collective-permute-start.4
  61.5 1.0 copy.43
  62.8 1.4 concatenate.82
  64.2 8.0 %collective-permute-done.4 = bf16[128,2,4,1,256]{4,2,0,1,3:T(4,128)(2,1)S(1)} collective-permute-done((bf16[128,2,4,1,256]{4,2,0,1,3:T(4,128)(2,1)}, bf16[128,2,4,1,256]{4,2,0,1,3:T(4,128)(2,1)S(1)}, u32[]{:S(2)}, u32[]{:S(2)}) %collective-permute-start.4) | collective-permute-done | bytes 524320 | tf_op jit(solution)/shard_map/ppermute | solution.py:8
  72.2 0.8 copy-done.2
  73.0 1.0 copy.44
  74.0 1.4 concatenate.83
  75.4 2.2 concatenate.87
  77.6 1.7 maximum_select_fusion.5
  79.6 1.5 maximum_maximum_fusion
  81.1 6.5 %collective-permute-done.1 = bf16[864,2,512]{2,0,1:T(8,128)(2,1)} collective-permute-done((bf16[864,2,512]{2,0,1:T(8,128)(2,1)S(1)}, bf16[864,2,512]{2,0,1:T(8,128)(2,1)}, u32[]{:S(2)}, u32[]{:S(2)}) %collective-permute-start.1) | collective-permute-done | bytes 1769504 | tf_op jit(solution)/shard_map/ppermute | solution.py:8
  87.6 3.2 maximum_select_fusion
  90.8 4.1 %copy.40 = bf16[864,2,1024]{0,2,1:T(8,128)(2,1)} copy(bf16[864,2,1024]{2,0,1:T(8,128)(2,1)S(1)} %maximum_select_fusion) | data formatting | bytes 7077888 | tf_op jit(solution)/shard_map/jit(_where)/select_n | solution.py:89
  94.9 6.1 %fusion.14 = f32[864,2,256]{2,0,1:T(8,128)} fusion(bf16[864,2048,1]{0,1,2:T(8,128)(2,1)} %bitcast.44, bf16[2,256,2048]{2,1,0:T(8,128)(2,1)} %bitcast.45), kind=kOutput, calls=%fused_computation.48 | convolution fusion | flops 1811939328 | bytes 7405568 | tf_op jit(solution)/shard_map/dot_general | solution.py:43
  101.1 74.0 %all-reduce.2.cloned.1.call-done = f32[864,2,256]{2,0,1:T(8,128)} async-done(((f32[864,2,256]{2,0,1:T(8,128)}), f32[864,2,256]{2,0,1:T(8,128)}) %all-reduce.2.cloned.1.call-update) | async-done | bytes 1769488 | tf_op jit(solution)/shard_map/psum | solution.py:93
  175.1 1.8 collective-permute-start.5
  176.9 36.9 %collective-permute-done.5 = f32[864,2,256]{2,0,1:T(8,128)S(1)} collective-permute-done((f32[864,2,256]{2,0,1:T(8,128)}, f32[864,2,256]{2,0,1:T(8,128)S(1)}, u32[]{:S(2)}, u32[]{:S(2)}) %collective-permute-start.5) | collective-permute-done | bytes 1769504 | tf_op jit(solution)/shard_map/ppermute | solution.py:8
  213.8 1.7 add.43
  215.6 3.1 collective-permute-start.6
  218.6 36.2 %collective-permute-done.6 = f32[864,2,256]{2,0,1:T(8,128)S(1)} collective-permute-done((f32[864,2,256]{2,0,1:T(8,128)S(1)}, f32[864,2,256]{2,0,1:T(8,128)S(1)}, u32[]{:S(2)}, u32[]{:S(2)}) %collective-permute-start.6) | collective-permute-done | bytes 1769504 | tf_op jit(solution)/shard_map/ppermute | solution.py:8
  254.8 1.5 add.44
  256.3 5.0 %collective-permute-start.7 = (f32[864,2,256]{2,0,1:T(8,128)}, f32[864,2,256]{2,0,1:T(8,128)}, u32[]{:S(2)}, u32[]{:S(2)}) collective-permute-start(f32[864,2,256]{2,0,1:T(8,128)} %add.44), channel_id=1, source_target_pairs={{0,4},{1,5},{2,6},{3,7},{4,0},{5,1},{6,2},{7,3},{8,12},{9,13},{10,... | collective-permute-start | bytes 5308424 | tf_op jit(solution)/shard_map/ppermute | solution.py:8
  261.3 0.6 copy.35
  261.9 0.9 reshape.118
  262.8 0.7 dot_general.22
  263.7 1.9 fusion.8
  265.6 2.0 copy.47
  267.6 66.9 %collective-permute-done.7 = f32[864,2,256]{2,0,1:T(8,128)} collective-permute-done((f32[864,2,256]{2,0,1:T(8,128)}, f32[864,2,256]{2,0,1:T(8,128)}, u32[]{:S(2)}, u32[]{:S(2)}) %collective-permute-start.7) | collective-permute-done | bytes 1769504 | tf_op jit(solution)/shard_map/ppermute | solution.py:8
  334.5 2.2 add.45
  336.7 2.6 copy.46
  339.3 3.6 reshape.120
  342.9 4.9 %convolution_convert_fusion = bf16[48,18,512]{2,1,0:T(8,128)(2,1)} fusion(f32[48,18,18]{2,1,0:T(8,128)} %copy.47, f32[48,18,512]{2,1,0:T(8,128)} %reshape.120), kind=kOutput, calls=%fused_computation.7 | convolution fusion | flops 95993856 | bytes 2716416 | tf_op jit(solution)/shard_map/aij,ajc->aic/dot_general | solution.py:33
  347.9 2.2 convert_element_type.12
  350.0 2.5 fusion.1
  352.6 1.3 fusion
  353.9 0.5 fusion.5
  354.7 0.4 select_n.250
  355.0 1.6 collective-permute-start.8
  357.0 7.3 %collective-permute-done.8 = bf16[128,2,4,1,256]{4,2,0,1,3:T(4,128)(2,1)S(1)} collective-permute-done((bf16[128,2,4,1,256]{4,2,0,1,3:T(4,128)(2,1)S(1)}, bf16[128,2,4,1,256]{4,2,0,1,3:T(4,128)(2,1)S(1)}, u32[]{:S(2)}, u32[]{:S(2)}) %collective-permute-start.8) | collective-permute-done | bytes 524320 | tf_op jit(solution)/shard_map/ppermute | solution.py:8
  364.3 0.8 maximum_select_fusion.6
  365.1 0.4 broadcast_select_fusion.5
  365.5 3.3 collective-permute-start.9
  368.8 7.7 %collective-permute-done.9 = bf16[64,2,4,2,256]{4,2,0,1,3:T(4,128)(2,1)S(1)} collective-permute-done((bf16[64,2,4,2,256]{4,2,0,1,3:T(4,128)(2,1)S(1)}, bf16[64,2,4,2,256]{4,2,0,1,3:T(4,128)(2,1)S(1)}, u32[]{:S(2)}, u32[]{:S(2)}) %collective-permute-start.9) | collective-permute-done | bytes 524320 | tf_op jit(solution)/shard_map/ppermute | solution.py:8
  376.5 1.2 maximum_select_fusion.7
  377.7 0.4 broadcast_select_fusion.9
  378.1 6.5 %collective-permute-start.10 = (bf16[32,2,4,4,256]{4,2,0,1,3:T(4,128)(2,1)S(1)}, bf16[32,2,4,4,256]{4,2,0,1,3:T(4,128)(2,1)S(1)}, u32[]{:S(2)}, u32[]{:S(2)}) collective-permute-start(bf16[32,2,4,4,256]{4,2,0,1,3:T(4,128)(2,1)S(1)} %get-tuple-element.8), channel_id=1, source_target_pairs={{0,4},{1,5},{2,6},{3,7},{4,0},{5,1},{6,2},{7,3},{8,12},{9,13},{10,... | collective-permute-start | bytes 1572872 | tf_op jit(solution)/shard_map/ppermute | solution.py:8
  384.6 18.0 %collective-permute-done.10 = bf16[32,2,4,4,256]{4,2,0,1,3:T(4,128)(2,1)S(1)} collective-permute-done((bf16[32,2,4,4,256]{4,2,0,1,3:T(4,128)(2,1)S(1)}, bf16[32,2,4,4,256]{4,2,0,1,3:T(4,128)(2,1)S(1)}, u32[]{:S(2)}, u32[]{:S(2)}) %collective-permute-start.10) | collective-permute-done | bytes 524320 | tf_op jit(solution)/shard_map/ppermute | solution.py:8
  402.5 1.2 maximum_select_fusion.8
  403.7 1.1 copy.48
  404.8 1.1 select_n.258
  (26 shorter events, 1.7 us)
Async XLA Ops:
  6.5 168.6 %all-reduce.2.cloned.1.call-start = ((), (), s32[]{:S(2)}) async-start(), calls=%async_computation | async-start | bytes 3538944 | tf_op jit(solution)/shard_map/psum | solution.py:93
  8.3 7.5 %copy-start.3 = (bf16[864,2,256]{2,1,0:T(2,128)(2,1)S(1)}, bf16[864,2,256]{2,1,0:T(2,128)(2,1)}, u32[]{:S(2)}) copy-start(bf16[864,2,256]{2,1,0:T(2,128)(2,1)} %param.6) | copy-start | bytes 2654212
  9.4 29.7 %collective-permute-start.2 = (bf16[32,2,4,4,256]{4,2,0,1,3:T(4,128)(2,1)S(1)}, bf16[32,2,4,4,256]{4,2,0,1,3:T(4,128)(2,1)S(1)}, u32[]{:S(2)}, u32[]{:S(2)}) collective-permute-start(bf16[32,2,4,4,256]{4,2,0,1,3:T(4,128)(2,1)S(1)} %get-tuple-element.20), channel_id=1, source_target_pairs={{0,4},{1,5},{2,6},{3,7},{4,0},{5,1},{6,2},{7,3},{8,12},{9,13},{10,... | collective-permute-start | bytes 1572872 | tf_op jit(solution)/shard_map/ppermute | solution.py:8
  15.9 28.8 %collective-permute-start = (bf16[864,2,256]{2,0,1:T(8,128)(2,1)S(1)}, bf16[864,2,256]{2,0,1:T(8,128)(2,1)}, u32[]{:S(2)}, u32[]{:S(2)}) collective-permute-start(bf16[864,2,256]{2,0,1:T(8,128)(2,1)S(1)} %copy.38), channel_id=1, source_target_pairs={{0,8},{1,9},{2,10},{3,11},{4,12},{5,13},{6,14},{7,15},{8,0},{9,1},... | collective-permute-start | bytes 2654216 | tf_op jit(solution)/shard_map/ppermute | solution.py:8
  41.5 14.8 %collective-permute-start.3 = (bf16[64,2,4,2,256]{4,2,0,1,3:T(4,128)(2,1)}, bf16[64,2,4,2,256]{4,2,0,1,3:T(4,128)(2,1)}, u32[]{:S(2)}, u32[]{:S(2)}) collective-permute-start(bf16[64,2,4,2,256]{4,2,0,1,3:T(4,128)(2,1)} %get-tuple-element.18), channel_id=1, source_target_pairs={{0,2},{1,3},{2,0},{3,1},{4,6},{5,7},{6,4},{7,5},{8,10},{9,11},{10,... | collective-permute-start | bytes 1572872 | tf_op jit(solution)/shard_map/ppermute | solution.py:8
  46.5 13.3 %copy-start = (bf16[864,2,512]{2,0,1:T(8,128)(2,1)}, bf16[864,2,512]{2,0,1:T(8,128)(2,1)S(1)}, u32[]{:S(2)}) copy-start(bf16[864,2,512]{2,0,1:T(8,128)(2,1)S(1)} %maximum_select_fusion.1) | copy-start | bytes 5308420
  46.6 41.1 %collective-permute-start.1 = (bf16[864,2,512]{2,0,1:T(8,128)(2,1)S(1)}, bf16[864,2,512]{2,0,1:T(8,128)(2,1)}, u32[]{:S(2)}, u32[]{:S(2)}) collective-permute-start(bf16[864,2,512]{2,0,1:T(8,128)(2,1)S(1)} %maximum_select_fusion.1), channel_id=1, source_target_pairs={{0,16},{1,17},{2,18},{3,19},{4,20},{5,21},{6,22},{7,23},{8,24},{9,... | collective-permute-start | bytes 5308424 | tf_op jit(solution)/shard_map/ppermute | solution.py:8
  59.9 12.3 %collective-permute-start.4 = (bf16[128,2,4,1,256]{4,2,0,1,3:T(4,128)(2,1)}, bf16[128,2,4,1,256]{4,2,0,1,3:T(4,128)(2,1)S(1)}, u32[]{:S(2)}, u32[]{:S(2)}) collective-permute-start(bf16[128,2,4,1,256]{4,2,0,1,3:T(4,128)(2,1)} %get-tuple-element.16), channel_id=1, source_target_pairs={{0,1},{1,0},{2,3},{3,2},{4,5},{5,4},{6,7},{7,6},{8,9},{9,8},{10,11... | collective-permute-start | bytes 1572872 | tf_op jit(solution)/shard_map/ppermute | solution.py:8
  72.2 0.8 copy-start.2
  79.6 8.0 %copy-start.1 = (bf16[864,2,512]{2,0,1:T(8,128)(2,1)S(1)}, bf16[864,2,512]{2,0,1:T(8,128)(2,1)}, u32[]{:S(2)}) copy-start(bf16[864,2,512]{2,0,1:T(8,128)(2,1)} %copy-done) | copy-start | bytes 5308420
  175.1 38.7 %collective-permute-start.5 = (f32[864,2,256]{2,0,1:T(8,128)}, f32[864,2,256]{2,0,1:T(8,128)S(1)}, u32[]{:S(2)}, u32[]{:S(2)}) collective-permute-start(f32[864,2,256]{2,0,1:T(8,128)} %all-reduce.2.cloned.1.call-done), channel_id=1, source_target_pairs={{0,1},{1,0},{2,3},{3,2},{4,5},{5,4},{6,7},{7,6},{8,9},{9,8},{10,11... | collective-permute-start | bytes 5308424 | tf_op jit(solution)/shard_map/ppermute | solution.py:8
  215.5 45.8 %copy-start.5 = (f32[4,18,18]{2,0,1:T(4,128)S(1)}, f32[4,18,18]{2,0,1:T(4,128)}, u32[]{:S(2)}) copy-start(f32[4,18,18]{2,0,1:T(4,128)} %param.7) | copy-start | bytes 15556
  215.5 48.0 %copy-start.6 = (s32[48]{0:T(128)S(1)}, s32[48]{0:T(128)}, u32[]{:S(2)}) copy-start(s32[48]{0:T(128)} %param.8) | copy-start | bytes 580
  215.5 48.0 %copy-start.7 = (s32[48]{0:T(128)S(1)}, s32[48]{0:T(128)}, u32[]{:S(2)}) copy-start(s32[48]{0:T(128)} %param.9) | copy-start | bytes 580
  215.6 39.2 %collective-permute-start.6 = (f32[864,2,256]{2,0,1:T(8,128)S(1)}, f32[864,2,256]{2,0,1:T(8,128)S(1)}, u32[]{:S(2)}, u32[]{:S(2)}) collective-permute-start(f32[864,2,256]{2,0,1:T(8,128)S(1)} %add.43), channel_id=1, source_target_pairs={{0,2},{1,3},{2,0},{3,1},{4,6},{5,7},{6,4},{7,5},{8,10},{9,11},{10,... | collective-permute-start | bytes 5308424 | tf_op jit(solution)/shard_map/ppermute | solution.py:8
  256.3 78.2 %collective-permute-start.7 = (f32[864,2,256]{2,0,1:T(8,128)}, f32[864,2,256]{2,0,1:T(8,128)}, u32[]{:S(2)}, u32[]{:S(2)}) collective-permute-start(f32[864,2,256]{2,0,1:T(8,128)} %add.44), channel_id=1, source_target_pairs={{0,4},{1,5},{2,6},{3,7},{4,0},{5,1},{6,2},{7,3},{8,12},{9,13},{10,... | collective-permute-start | bytes 5308424 | tf_op jit(solution)/shard_map/ppermute | solution.py:8
  350.0 2.5 copy-start.4
  355.0 9.3 %collective-permute-start.8 = (bf16[128,2,4,1,256]{4,2,0,1,3:T(4,128)(2,1)S(1)}, bf16[128,2,4,1,256]{4,2,0,1,3:T(4,128)(2,1)S(1)}, u32[]{:S(2)}, u32[]{:S(2)}) collective-permute-start(bf16[128,2,4,1,256]{4,2,0,1,3:T(4,128)(2,1)S(1)} %select_n.250), channel_id=1, source_target_pairs={{0,1},{1,0},{2,3},{3,2},{4,5},{5,4},{6,7},{7,6},{8,9},{9,8},{10,11... | collective-permute-start | bytes 1572872 | tf_op jit(solution)/shard_map/ppermute | solution.py:8
  365.5 11.0 %collective-permute-start.9 = (bf16[64,2,4,2,256]{4,2,0,1,3:T(4,128)(2,1)S(1)}, bf16[64,2,4,2,256]{4,2,0,1,3:T(4,128)(2,1)S(1)}, u32[]{:S(2)}, u32[]{:S(2)}) collective-permute-start(bf16[64,2,4,2,256]{4,2,0,1,3:T(4,128)(2,1)S(1)} %get-tuple-element.10), channel_id=1, source_target_pairs={{0,2},{1,3},{2,0},{3,1},{4,6},{5,7},{6,4},{7,5},{8,10},{9,11},{10,... | collective-permute-start | bytes 1572872 | tf_op jit(solution)/shard_map/ppermute | solution.py:8
  378.1 24.5 %collective-permute-start.10 = (bf16[32,2,4,4,256]{4,2,0,1,3:T(4,128)(2,1)S(1)}, bf16[32,2,4,4,256]{4,2,0,1,3:T(4,128)(2,1)S(1)}, u32[]{:S(2)}, u32[]{:S(2)}) collective-permute-start(bf16[32,2,4,4,256]{4,2,0,1,3:T(4,128)(2,1)S(1)} %get-tuple-element.8), channel_id=1, source_target_pairs={{0,4},{1,5},{2,6},{3,7},{4,0},{5,1},{6,2},{7,3},{8,12},{9,13},{10,... | collective-permute-start | bytes 1572872 | tf_op jit(solution)/shard_map/ppermute | solution.py:8
Sparse Core Ops, SparseCore 0:
  101.2 73.8 all-reduce.1
where the time goes:
time: 417 us; the launch traced here: 413 us
  waiting for transfers between devices  290 us (70%)
  starting transfers between devices  37.1 us (9%)
  local copies, waits for them, and re-layouts  30.3 us (7%)
  other arithmetic  25.3 us (6%)
  matrix products  16.8 us (4%)
  between operations  13.6 us (3%)
    ppermute x11, waiting for transfers between devices, swapped(): lax.ppermute(array, axis, [(i, i ^ 1 << apart) for i in range(lax.axis_si...  216 us
    psum x1, waiting for transfers between devices, grid_apply(): becp = lax.psum(partial_value, 'ga')  74 us
    ppermute x11, starting transfers between devices, swapped(): lax.ppermute(array, axis, [(i, i ^ 1 << apart) for i in range(lax.axis_si...  37.1 us
  transfers between devices with their start and end apart: 12, of which 11 were waited for; matrix products, arithmetic and copies ran while one was open for 6% of the time, Pallas kernels for 0%

commit v1 on v0

v1 whole, which is shorter than its diff:
```python
import jax
import jax.numpy as jnp
from jax import lax
from jax.experimental import pallas as pl
from jax.experimental.pallas import tpu as pltpu
from jax.sharding import PartitionSpec as P

NX, NY, NH, NZ, NC = 4, 4, 2, 4, 2
XY = NX * NY
PER_ATOM = 18
GROUP_ATOMS = 14
GROUPS = ((0, 256), (256, 256), (512, 256), (768, 128))
WIDTH = 256
ROWS = 896
HIGHEST = lax.Precision.HIGHEST
NT = (((1,), (1,)), ((), ()))
NN = (((1,), (0,)), ((), ()))


def coupling_matrix(group, cpad, species, offsets):
    row = lax.broadcasted_iota(jnp.int32, (256, 1), 0)
    row_atom = (row * 3641) >> 16
    row_in = row - row_atom * PER_ATOM
    start = (row_atom + GROUP_ATOMS * group) * PER_ATOM
    kind = jnp.sum(
        jnp.where(offsets == start, species.astype(jnp.float32), 0.0), axis=1, keepdims=True
    )
    col = lax.broadcasted_iota(jnp.int32, (256, 128), 1)
    col_kind = (col * 3641) >> 16
    col_in = col - col_kind * PER_ATOM
    pick = jnp.where(
        (col_kind.astype(jnp.float32) == kind) & (col_in == row_in), 1.0, 0.0
    ).astype(jnp.float32)
    rows = lax.dot_general(pick, cpad, NN, precision=HIGHEST, preferred_element_type=jnp.float32)
    wide = lax.broadcasted_iota(jnp.int32, (128, 256), 1)
    wide_atom = (wide * 3641) >> 16
    spread = jnp.where(
        wide - wide_atom * PER_ATOM == lax.broadcasted_iota(jnp.int32, (128, 256), 0), 1.0, 0.0
    ).astype(jnp.float32)
    full = lax.dot_general(rows, spread, NN, precision=HIGHEST, preferred_element_type=jnp.float32)
    full_row = lax.broadcasted_iota(jnp.int32, (256, 256), 0)
    full_col = lax.broadcasted_iota(jnp.int32, (256, 256), 1)
    same = ((full_row * 3641) >> 16) == ((full_col * 3641) >> 16)
    return jnp.where(same, full, 0.0)


def turn_matrix():
    row = lax.broadcasted_iota(jnp.int32, (256, 256), 0)
    col = lax.broadcasted_iota(jnp.int32, (256, 256), 1)
    even = (row & 1) == 0
    up = even & (col == row + 1)
    down = jnp.logical_not(even) & (col == row - 1)
    return (jnp.where(up, 1.0, 0.0) - jnp.where(down, 1.0, 0.0)).astype(jnp.bfloat16)


def kernel(
    orb, proj, coup, species, offsets, out,
    pz, pd, pf, xt, xj, jm, cm, cpad, sb, rb, town, zs, zr, dg, dj, acc, ab,
    pz_s, pz_r, pd_s, pd_r, pf_s, pf_r, o_s, o_r, rs_s, rs_r, z_s, z_r, ag_s, ag_r, b_s, b_r, loc_s,
):
    ga = lax.axis_index("ga")
    band = lax.axis_index("band")
    zl, core = ga // NC, ga % NC
    x, h, y = band // (NH * NY), band // NY % NH, band % NY
    me = x * NY + y

    def xy_band(k):
        return k // NY * (NH * NY) + h * NY + k % NY

    def copy(src, dst, send, recv, to_ga, to_band):
        return pltpu.make_async_remote_copy(
            src_ref=src, dst_ref=dst, send_sem=send, recv_sem=recv,
            device_id={"ga": to_ga, "band": to_band},
            device_id_type=pl.DeviceIdType.MESH,
        )

    def arrived(ref, sem):
        copy(ref, ref, sem, sem, ga, band).wait_recv()

    def left(ref, sem):
        copy(ref, ref, sem, sem, ga, band).wait_send()

    other_core = zl * NC + 1 - core
    other_half = band + NY - 2 * NY * h

    barrier = pltpu.get_barrier_semaphore()

    def greet(to_ga, to_band):
        pl.semaphore_signal(
            barrier, inc=1, device_id={"ga": to_ga, "band": to_band},
            device_id_type=pl.DeviceIdType.MESH,
        )

    greet(ga, other_half)
    for c in range(1, NZ):
        greet((zl + c) % NZ * NC + core, band)
    greet(other_core, band)

    def greet_plane(d, _):
        k = (me + d) % XY
        greet(ga, xy_band(k))
        greet(other_core, xy_band(k))
        return 0

    lax.fori_loop(1, XY, greet_plane, 0)
    pl.semaphore_wait(barrier, 1 + (NZ - 1) + 1 + 2 * (XY - 1))

    def z_copy(k):
        rows = pl.ds(GROUPS[k][0], GROUPS[k][1])
        return copy(proj.at[rows], pz.at[rows], pz_s.at[k], pz_r.at[k], ga, other_half)

    def fwd_copy(k):
        rows = pl.ds(GROUPS[k][0], GROUPS[k][1])
        return copy(pz.at[rows], pf.at[rows], pf_s.at[k], pf_r.at[k], other_core, band)

    z_copy(0).start()
    z_copy(1).start()
    own_copy = copy(proj, pd, pd_s, pd_r, other_core, band)
    own_copy.start()

    def orb_copy(k, c):
        return copy(
            orb.at[k // NY, :, k % NY, pl.ds(32 * c, 32), :],
            xt.at[core, :, pl.ds(32 * me, 32), :],
            o_s, o_r.at[core], zl * NC + c, xy_band(k),
        )

    def orb_send(d, _):
        k = (me + d) % XY
        orb_copy(k, core).start()
        orb_copy(k, 1 - core).start()
        return 0

    lax.fori_loop(1, XY, orb_send, 0)
    orb_copy(me, 1 - core).start()
    for q in range(NH):
        xt[core, q, pl.ds(32 * me, 32), :] = orb[x, q, y, pl.ds(32 * core, 32), :]

    jm[...] = turn_matrix()
    cpad[...] = jnp.zeros_like(cpad)
    for s in range(4):
        cpad[pl.ds(PER_ATOM * s, PER_ATOM), pl.ds(0, PER_ATOM)] = coup[s]
    for k in range(4):
        cm[k] = coupling_matrix(k, cpad[...], species[...], offsets[...])

    arrived(xt.at[core, :, pl.ds(0, 480), :], o_r.at[core])
    arrived(xt.at[1 - core], o_r.at[1 - core])

    def turn(i, _):
        g, q, r = i // 4, i // 2 % 2, i % 2
        rows = pl.ds(256 * r, 256)
        xj[g, q, rows, :] = lax.dot_general(
            jm[...], xt[g, q, rows, :], NN, preferred_element_type=jnp.float32
        ).astype(jnp.bfloat16)
        return 0

    lax.fori_loop(0, 8, turn, 0)
    arrived(pd, pd_r)

    pieces = ((proj, core, h), (pz, core, 1 - h), (pd, 1 - core, h), (pf, 1 - core, 1 - h))

    def first_product(k):
        start, n = GROUPS[k]

        def block(r, _):
            rows = pl.ds(256 * r, 256)
            total = None
            for ref, g, q in pieces:
                re = lax.dot_general(
                    xt[g, q, rows, :], ref[pl.ds(start, n), pl.ds(0, 256)], NT,
                    preferred_element_type=jnp.float32,
                )
                im = lax.dot_general(
                    xj[g, q, rows, :], ref[pl.ds(start, n), pl.ds(256, 256)], NT,
                    preferred_element_type=jnp.float32,
                )
                total = re + im if total is None else total + re + im
            sb[k, rows, pl.ds(0, n)] = total.astype(jnp.bfloat16)
            return 0

        lax.fori_loop(0, 2, block, 0)

    def rs_send(k):
        n = GROUPS[k][1]

        def one(d, _):
            to = (me + d) % XY
            copy(
                sb.at[k, pl.ds(32 * to, 32), pl.ds(0, n)],
                rb.at[k, XY - 1 - d, :, pl.ds(0, n)],
                rs_s.at[k], rs_r.at[k], ga, xy_band(to),
            ).start()
            return 0

        lax.fori_loop(1, XY, one, 0)

    def z_sum(k):
        n = GROUPS[k][1]
        arrived(rb.at[k, :, :, pl.ds(0, n)], rs_r.at[k])
        total = sb[k, pl.ds(32 * me, 32), pl.ds(0, n)].astype(jnp.float32)
        for d in range(XY - 1):
            total = total + rb[k, d, :, pl.ds(0, n)].astype(jnp.float32)
        town[k, :, pl.ds(0, n)] = total
        zs[k, :, pl.ds(0, n)] = total.astype(jnp.bfloat16)
        for c in range(1, NZ):
            to = (zl + c) % NZ
            copy(
                zs.at[k, :, pl.ds(0, n)], zr.at[k, NZ - 1 - c, :, pl.ds(0, n)],
                z_s.at[k], z_r.at[k], to * NC + core, band,
            ).start()

    def couple(k):
        n = GROUPS[k][1]
        arrived(zr.at[k, :, :, pl.ds(0, n)], z_r.at[k])
        total = town[k, :, pl.ds(0, n)]
        for c in range(NZ - 1):
            total = total + zr[k, c, :, pl.ds(0, n)].astype(jnp.float32)
        coupled = lax.dot_general(
            total, cm[k, pl.ds(0, n), pl.ds(0, n)], NT, precision=HIGHEST,
            preferred_element_type=jnp.float32,
        )
        mine = pl.ds(32 * me, 32)
        dg[k, mine, pl.ds(0, n)] = coupled.astype(jnp.bfloat16)

        def one(d, _):
            to = (me + d) % XY
            part = dg.at[k, mine, pl.ds(0, n)]
            copy(part, part, ag_s.at[k], ag_r.at[k], ga, xy_band(to)).start()
            return 0

        lax.fori_loop(1, XY, one, 0)

    def gather(k):
        n = GROUPS[k][1]
        arrived(dg.at[k, pl.ds(0, 480), pl.ds(0, n)], ag_r.at[k])

        def block(r, _):
            rows = pl.ds(256 * r, 256)
            dj[k, rows, pl.ds(0, n)] = (
                -lax.dot_general(
                    jm[...], dg[k, rows, pl.ds(0, n)], NN, preferred_element_type=jnp.float32
                )
            ).astype(jnp.bfloat16)
            return 0

        lax.fori_loop(0, 2, block, 0)

    def second_product(groups, first, last):
        for ref, g, q in pieces:

            def block(r, _):
                rows = pl.ds(256 * r, 256)
                total = None
                for k in groups:
                    start, n = GROUPS[k]
                    re = lax.dot_general(
                        dg[k, rows, pl.ds(0, n)], ref[pl.ds(start, n), pl.ds(0, 256)], NN,
                        preferred_element_type=jnp.float32,
                    )
                    im = lax.dot_general(
                        dj[k, rows, pl.ds(0, n)], ref[pl.ds(start, n), pl.ds(256, 256)], NN,
                        preferred_element_type=jnp.float32,
                    )
                    total = re + im if total is None else total + re + im
                if not first:
                    total = total + acc[g, q, rows, :]
                if last:
                    ab[g, q, rows, :] = total.astype(jnp.bfloat16)
                else:
                    acc[g, q, rows, :] = total
                return 0

            lax.fori_loop(0, 2, block, 0)

    for k in range(4):
        z_copy(k).wait_recv()
        fwd_copy(k).start()
        z_copy(k).wait_send()
        if k + 2 < 4:
            z_copy(k + 2).start()
        fwd_copy(k).wait_recv()
        first_product(k)
        rs_send(k)
        if k >= 1:
            z_sum(k - 1)
        if k >= 2:
            couple(k - 2)
    couple(2)
    gather(0)
    gather(1)
    second_product((0, 1), True, False)
    z_sum(3)
    gather(2)
    second_product((2,), False, False)
    couple(3)
    gather(3)
    second_product((3,), False, True)

    def back_copy(k, c):
        return copy(
            ab.at[c, :, pl.ds(32 * k, 32), :],
            out.at[x, :, y, pl.ds(32 * core, 32), :],
            b_s, b_r.at[core], zl * NC + c, xy_band(k),
        )

    def back_send(d, _):
        k = (me + d) % XY
        back_copy(k, core).start()
        back_copy(k, 1 - core).start()
        return 0

    lax.fori_loop(1, XY, back_send, 0)
    back_copy(me, 1 - core).start()
    local = pltpu.make_async_copy(
        ab.at[core, :, pl.ds(32 * me, 32), :], out.at[x, :, y, pl.ds(32 * core, 32), :], loc_s
    )
    local.start()

    left(proj, pd_s)
    for k in range(4):
        n = GROUPS[k][1]
        fwd_copy(k).wait_send()
        left(rb.at[k, :, :, pl.ds(0, n)], rs_s.at[k])
        left(zr.at[k, :, :, pl.ds(0, n)], z_s.at[k])
        left(dg.at[k, pl.ds(0, 480), pl.ds(0, n)], ag_s.at[k])
    left(xt.at[0], o_s)
    left(xt.at[0, :, pl.ds(0, 480), :], o_s)
    left(ab.at[0], b_s)
    left(ab.at[0, :, pl.ds(0, 480), :], b_s)
    local.wait()
    arrived(ab.at[core, :, pl.ds(0, 480), :], b_r.at[core])
    arrived(ab.at[1 - core], b_r.at[1 - core])


def per_device(orbitals, projectors, coupling, species, offsets):
    bf16, f32 = jnp.bfloat16, jnp.float32
    bands = orbitals.shape[0]
    orb = orbitals.reshape(bands, 2, NX, NH, NY, WIDTH).transpose(2, 3, 4, 0, 1, 5)
    orb = orb.reshape(NX, NH, NY, 2 * bands, WIDTH)
    flat = projectors.reshape(projectors.shape[0], 2 * WIDTH)
    step = GROUP_ATOMS * PER_ATOM
    parts = []
    for k in range(4):
        part = flat[step * k : step * (k + 1)]
        parts.append(jnp.pad(part, ((0, GROUPS[k][1] - part.shape[0]), (0, 0))))
    proj = jnp.concatenate(parts, axis=0)
    vmem = pl.BlockSpec(memory_space=pltpu.VMEM)
    dma = pltpu.SemaphoreType.DMA
    out = pl.pallas_call(
        kernel,
        out_shape=jax.ShapeDtypeStruct(orb.shape, bf16),
        in_specs=[vmem] * 5,
        out_specs=pl.BlockSpec(memory_space=pl.ANY),
        scratch_shapes=[
            pltpu.VMEM((ROWS, 512), bf16),
            pltpu.VMEM((ROWS, 512), bf16),
            pltpu.VMEM((ROWS, 512), bf16),
            pltpu.VMEM((2, 2, 512, 256), bf16),
            pltpu.VMEM((2, 2, 512, 256), bf16),
            pltpu.VMEM((256, 256), bf16),
            pltpu.VMEM((4, 256, 256), f32),
            pltpu.VMEM((128, 128), f32),
            pltpu.VMEM((4, 512, 256), bf16),
            pltpu.VMEM((4, XY - 1, 32, 256), bf16),
            pltpu.VMEM((4, 32, 256), f32),
            pltpu.VMEM((4, 32, 256), bf16),
            pltpu.VMEM((4, NZ - 1, 32, 256), bf16),
            pltpu.VMEM((4, 512, 256), bf16),
            pltpu.VMEM((4, 512, 256), bf16),
            pltpu.VMEM((2, 2, 512, 256), f32),
            pltpu.VMEM((2, 2, 512, 256), bf16),
            dma((4,)), dma((4,)), dma, dma, dma((4,)), dma((4,)),
            dma, dma((2,)), dma((4,)), dma((4,)), dma((4,)), dma((4,)),
            dma((4,)), dma((4,)), dma, dma((2,)), dma,
        ],
        compiler_params=pltpu.CompilerParams(collective_id=0, has_side_effects=True),
    )(orb, proj, coupling, species.reshape(1, -1), offsets.reshape(1, -1))
    out = out.reshape(NX, NH, NY, bands, 2, WIDTH).transpose(3, 4, 0, 1, 2, 5)
    return out.reshape(orbitals.shape)


def solution(mesh):
    placed = (P("band", None, "ga"), P(None, None, ("ga", "band")), P(), P(), P())
    return jax.shard_map(
        per_device, mesh=mesh, in_specs=placed, out_specs=P("band", None, "ga"), check_vma=False
    )
```

time: 417 us -> 110 us (0.26)
  the two profiles are of different devices: /device:TPU:32 before, /device:TPU:57 now
where the time goes in v1:
time: 110 us
  Pallas kernels  96.7 us (88%)
  local copies, waits for them, and re-layouts  12 us (11%)
    pallas_call x1, Pallas kernels, per_device(): pl.pallas_call(kernel, out_shape=jax.ShapeDtypeStruct(orb.shape, bf16), i...  96.7 us
    slice x2, local copies, waits for them, and re-layouts, per_device(): part = flat[step * k:step * (k + 1)]  2.71 us
    unnamed x11, local copies, waits for them, and re-layouts  2.68 us

profile of v1, /device:TPU:57, one launch (start us, length us, event | category | flops | bytes accessed | tf_op | source)
XLA Modules:
  0.0 109.8 jit_solution(16695506173151671213)
XLA Ops:
  0.0 1.4 %copy.7.coup = f32[4,18,18]{2,1,0:T(8,128)} copy(f32[4,18,18]{2,0,1:T(4,128)} %param.7) | data formatting | bytes 10368 | tf_op args[2]
  1.4 1.0 slice.30
  2.4 0.1 pad.29
  2.5 1.7 %fusion.9 = (bf16[252,2,256]{2,1,0:T(2,128)(2,1)S(1)}, bf16[252,2,256]{2,1,0:T(2,128)(2,1)S(1)}, bf16[252,2,256]{2,1,0:T(2,128)(2,1)S(1)}) fusion(bf16[864,2,256]{2,1,0:T(2,128)(2,1)} %param.6), kind=kLoop, calls=%fused_computation.16 | loop fusion | bytes 1548288 | tf_op jit(solution)/shard_map/slice | solution.py:344
  4.2 0.2 pad.26
  4.5 0.2 pad.27
  4.7 0.2 pad.28
  4.9 0.0 copy-start
  5.0 1.0 fusion.7.proj
  6.0 0.5 copy-done
  6.5 0.8 reshape.23
  7.3 1.1 copy.14
  8.4 1.2 %reshape.24.orb = bf16[4,2,4,64,256]{4,3,2,1,0:T(8,128)(2,1)} reshape(bf16[4,2,4,32,2,256]{5,4,3,2,1,0:T(2,128)(2,1)S(1)} %bitcast.20) | data formatting | bytes 2097152 | tf_op jit(solution)/shard_map/reshape | solution.py:339
  9.6 96.7 %shard_map.55 = bf16[4,2,4,64,256]{4,3,2,1,0:T(8,128)(2,1)} custom-call(bf16[4,2,4,64,256]{4,3,2,1,0:T(8,128)(2,1)} %reshape.24.orb, bf16[896,512]{1,0:T(8,128)(2,1)} %fusion.7.proj, f32[4,18,18]{2,1,0:T(8,128)} %copy.7.coup, s32[1,48]{1,0:T(1,128)} %bitcast.30, s32[1,48]{1,0:T(1,128)} %bitcast.31), custom_call_target="tpu_custom_call" | custom-call | tf_op jit(solution)/shard_map/pallas_call | solution.py:349
  106.3 1.5 %reshape.27 = bf16[4,2,4,32,2,256]{5,4,3,2,1,0:T(2,128)(2,1)S(1)} reshape(bf16[4,2,4,64,256]{4,3,2,1,0:T(8,128)(2,1)} %shard_map.55) | data formatting | bytes 2097152 | tf_op jit(solution)/shard_map/reshape | solution.py:378
  107.8 0.8 copy.8
  108.6 1.2 %reshape.28 = bf16[32,2,8192]{2,1,0:T(2,128)(2,1)} reshape(bf16[32,2,4,2,4,256]{5,4,3,2,1,0:T(4,128)(2,1)S(1)} %copy.8) | data formatting | bytes 2097152 | tf_op jit(solution)/shard_map/reshape | solution.py:379
  (4 shorter events, 0.1 us)
Async XLA Ops:
  4.9 1.6 %copy-start = (bf16[32,2,8192]{2,1,0:T(2,128)(2,1)S(1)}, bf16[32,2,8192]{2,1,0:T(2,128)(2,1)}, u32[]{:S(2)}) copy-start(bf16[32,2,8192]{2,1,0:T(2,128)(2,1)} %param.5) | copy-start | bytes 3145732

commit v2 on v1

v2 whole, which is shorter than its diff:
```python
import jax
import jax.numpy as jnp
from jax import lax
from jax.experimental import pallas as pl
from jax.experimental.pallas import tpu as pltpu
from jax.sharding import PartitionSpec as P

NX, NY, NH, NZ, NC = 4, 4, 2, 4, 2
XY = NX * NY
PER_ATOM = 18
GROUP_ATOMS = 14
GROUPS = ((0, 256), (256, 256), (512, 256), (768, 128))
WIDTH = 256
ROWS = 896
COUNTS = (252, 252, 252, 108)
HIGHEST = lax.Precision.HIGHEST
NT = (((1,), (1,)), ((), ()))
NN = (((1,), (0,)), ((), ()))


def coupling_matrix(group, cpad, species, offsets):
    row = lax.broadcasted_iota(jnp.int32, (256, 1), 0)
    row_atom = (row * 3641) >> 16
    row_in = row - row_atom * PER_ATOM
    start = (row_atom + GROUP_ATOMS * group) * PER_ATOM
    kind = jnp.sum(
        jnp.where(offsets == start, species.astype(jnp.float32), 0.0), axis=1, keepdims=True
    )
    col = lax.broadcasted_iota(jnp.int32, (256, 128), 1)
    col_in, col_kind = col >> 2, col & 3
    pick = jnp.where(
        (col_kind.astype(jnp.float32) == kind) & (col_in == row_in), 1.0, 0.0
    ).astype(jnp.float32)
    rows = lax.dot_general(pick, cpad, NN, precision=HIGHEST, preferred_element_type=jnp.float32)
    wide = lax.broadcasted_iota(jnp.int32, (128, 256), 1)
    wide_atom = (wide * 3641) >> 16
    spread = jnp.where(
        wide - wide_atom * PER_ATOM == lax.broadcasted_iota(jnp.int32, (128, 256), 0), 1.0, 0.0
    ).astype(jnp.float32)
    full = lax.dot_general(rows, spread, NN, precision=HIGHEST, preferred_element_type=jnp.float32)
    full_row = lax.broadcasted_iota(jnp.int32, (256, 256), 0)
    full_col = lax.broadcasted_iota(jnp.int32, (256, 256), 1)
    same = ((full_row * 3641) >> 16) == ((full_col * 3641) >> 16)
    return jnp.where(same, full, 0.0)


def turn_matrix():
    row = lax.broadcasted_iota(jnp.int32, (256, 256), 0)
    col = lax.broadcasted_iota(jnp.int32, (256, 256), 1)
    even = (row & 1) == 0
    up = even & (col == row + 1)
    down = jnp.logical_not(even) & (col == row - 1)
    return (jnp.where(up, 1.0, 0.0) - jnp.where(down, 1.0, 0.0)).astype(jnp.bfloat16)


def split_matrix():
    row = lax.broadcasted_iota(jnp.int32, (256, 256), 0)
    col = lax.broadcasted_iota(jnp.int32, (256, 256), 1)
    return jnp.where(col == (row & 127) * 2 + (row >> 7), 1.0, 0.0).astype(jnp.bfloat16)


def kernel(
    orb, proj, coup, species, offsets, out,
    praw, pc, xr, xt, xj, jm, pm, cm, cpad, sb, rb, town, zs, zr, dg, dj, acc, ab,
    pz_s, pz_r, pd_s, pd_r, pf_s, pf_r, o_s, o_r, rs_s, rs_r, z_s, z_r, ag_s, ag_r, b_s, b_r,
    own_s, oo_s, loc_s,
):
    ga = lax.axis_index("ga")
    band = lax.axis_index("band")
    zl, core = ga // NC, ga % NC
    x, h, y = band // (NH * NY), band // NY % NH, band % NY
    me = x * NY + y

    def xy_band(k):
        return k // NY * (NH * NY) + h * NY + k % NY

    def copy(src, dst, send, recv, to_ga, to_band):
        return pltpu.make_async_remote_copy(
            src_ref=src, dst_ref=dst, send_sem=send, recv_sem=recv,
            device_id={"ga": to_ga, "band": to_band},
            device_id_type=pl.DeviceIdType.MESH,
        )

    def arrived(ref, sem):
        copy(ref, ref, sem, sem, ga, band).wait_recv()

    def left(ref, sem):
        copy(ref, ref, sem, sem, ga, band).wait_send()

    other_core = zl * NC + 1 - core
    other_half = band + NY - 2 * NY * h

    barrier = pltpu.get_barrier_semaphore()

    def part(k):
        return pl.ds(GROUPS[k][0], COUNTS[k])

    def source(k):
        return proj.at[pl.ds(GROUP_ATOMS * PER_ATOM * k, COUNTS[k])]

    def columns(k, q):
        block = k // NY * (NH * NY) + q * NY + k % NY
        return pl.ds(pl.multiple_of(WIDTH * block, WIDTH), WIDTH)

    def greet(to_ga, to_band):
        pl.semaphore_signal(
            barrier, inc=1, device_id={"ga": to_ga, "band": to_band},
            device_id_type=pl.DeviceIdType.MESH,
        )

    greet(ga, other_half)
    for c in range(1, NZ):
        greet((zl + c) % NZ * NC + core, band)
    greet(other_core, band)

    def greet_plane(d, _):
        k = (me + d) % XY
        greet(ga, xy_band(k))
        greet(other_core, xy_band(k))
        return 0

    lax.fori_loop(1, XY, greet_plane, 0)
    own = [pltpu.make_async_copy(source(k), praw.at[0, part(k)], own_s.at[k]) for k in range(4)]
    for k in range(4):
        own[k].start()

    def z_copy(k):
        return copy(source(k), praw.at[1, part(k)], pz_s.at[k], pz_r.at[k], ga, other_half)

    def core_copy(k):
        return copy(source(k), praw.at[2, part(k)], pd_s.at[k], pd_r.at[k], other_core, band)

    def fwd_copy(k):
        return copy(
            praw.at[1, part(k)], praw.at[3, part(k)], pf_s.at[k], pf_r.at[k], other_core, band
        )

    for piece in range(4):
        for k in range(4):
            pad = GROUPS[k][1] - COUNTS[k]
            praw[piece, pl.ds(GROUPS[k][0] + COUNTS[k], pad)] = jnp.zeros(
                (pad, 2, WIDTH), jnp.bfloat16
            )

    pl.semaphore_wait(barrier, 1 + (NZ - 1) + 1 + 2 * (XY - 1))
    z_copy(0).start()
    z_copy(1).start()

    def orb_copy(k, c, q):
        return copy(
            orb.at[pl.ds(16 * c, 16), :, columns(k, q)],
            xr.at[core, q, pl.ds(16 * me, 16)],
            o_s, o_r.at[core], zl * NC + c, xy_band(k),
        )

    def orb_send(d, _):
        k = (me + d) % XY
        for q in range(NH):
            orb_copy(k, core, q).start()
            orb_copy(k, 1 - core, q).start()
        return 0

    lax.fori_loop(1, XY, orb_send, 0)
    own_orb = []
    for q in range(NH):
        orb_copy(me, 1 - core, q).start()
        own_orb.append(
            pltpu.make_async_copy(
                orb.at[pl.ds(16 * core, 16), :, columns(me, q)],
                xr.at[core, q, pl.ds(16 * me, 16)],
                oo_s.at[q],
            )
        )
        own_orb[q].start()
    for k in range(4):
        core_copy(k).start()

    jm[...] = turn_matrix()
    pm[...] = split_matrix()
    cpad[...] = jnp.zeros_like(cpad)
    for i in range(PER_ATOM):
        cpad[pl.ds(4 * i, 4), pl.ds(0, PER_ATOM)] = coup[i]
    for k in range(4):
        cm[k] = coupling_matrix(k, cpad[...], species[...], offsets[...])

    for k in range(4):
        own[k].wait()
        core_copy(k).wait_recv()

    def split(k, piece):
        start, n = GROUPS[k]

        def block(i, _):
            at = pl.multiple_of(start + 128 * i, 128)
            both = lax.dot_general(
                pm[...], praw[piece, pl.ds(at, 128)].reshape(256, WIDTH), NN,
                preferred_element_type=jnp.float32,
            ).astype(jnp.bfloat16)
            pc[piece, 0, pl.ds(at, 128), :] = both[:128]
            pc[piece, 1, pl.ds(at, 128), :] = both[128:]
            return 0

        lax.fori_loop(0, n // 128, block, 0)

    for k in range(4):
        split(k, 0)
        split(k, 2)

    for q in range(NH):
        own_orb[q].wait()
    arrived(xr.at[core, :, pl.ds(0, 240)], o_r.at[core])
    arrived(xr.at[1 - core], o_r.at[1 - core])

    def turn(i, _):
        g, q, r = i // 4, i // 2 % 2, i % 2
        rows = pl.ds(pl.multiple_of(256 * r, 256), 256)
        value = xr[g, q, pl.ds(pl.multiple_of(128 * r, 128), 128)].reshape(256, WIDTH)
        xt[g, q, rows, :] = value
        xj[g, q, rows, :] = lax.dot_general(
            jm[...], value, NN, preferred_element_type=jnp.float32
        ).astype(jnp.bfloat16)
        return 0

    lax.fori_loop(0, 8, turn, 0)

    pieces = ((0, core, h), (1, core, 1 - h), (2, 1 - core, h), (3, 1 - core, 1 - h))

    def first_product(k):
        start, n = GROUPS[k]

        def block(r, _):
            rows = pl.ds(256 * r, 256)
            total = None
            for i, g, q in pieces:
                re = lax.dot_general(
                    xt[g, q, rows, :], pc[i, 0, pl.ds(start, n), :], NT,
                    preferred_element_type=jnp.float32,
                )
                im = lax.dot_general(
                    xj[g, q, rows, :], pc[i, 1, pl.ds(start, n), :], NT,
                    preferred_element_type=jnp.float32,
                )
                total = re + im if total is None else total + re + im
            sb[k, rows, pl.ds(0, n)] = total.astype(jnp.bfloat16)
            return 0

        lax.fori_loop(0, 2, block, 0)

    def rs_send(k):
        n = GROUPS[k][1]

        def one(d, _):
            to = (me + d) % XY
            copy(
                sb.at[k, pl.ds(32 * to, 32), pl.ds(0, n)],
                rb.at[k, XY - 1 - d, :, pl.ds(0, n)],
                rs_s.at[k], rs_r.at[k], ga, xy_band(to),
            ).start()
            return 0

        lax.fori_loop(1, XY, one, 0)

    def z_sum(k):
        n = GROUPS[k][1]
        arrived(rb.at[k, :, :, pl.ds(0, n)], rs_r.at[k])
        total = sb[k, pl.ds(32 * me, 32), pl.ds(0, n)].astype(jnp.float32)
        for d in range(XY - 1):
            total = total + rb[k, d, :, pl.ds(0, n)].astype(jnp.float32)
        town[k, :, pl.ds(0, n)] = total
        zs[k, :, pl.ds(0, n)] = total.astype(jnp.bfloat16)
        for c in range(1, NZ):
            to = (zl + c) % NZ
            copy(
                zs.at[k, :, pl.ds(0, n)], zr.at[k, NZ - 1 - c, :, pl.ds(0, n)],
                z_s.at[k], z_r.at[k], to * NC + core, band,
            ).start()

    def couple(k):
        n = GROUPS[k][1]
        arrived(zr.at[k, :, :, pl.ds(0, n)], z_r.at[k])
        total = town[k, :, pl.ds(0, n)]
        for c in range(NZ - 1):
            total = total + zr[k, c, :, pl.ds(0, n)].astype(jnp.float32)
        coupled = lax.dot_general(
            total, cm[k, pl.ds(0, n), pl.ds(0, n)], NT, precision=HIGHEST,
            preferred_element_type=jnp.float32,
        )
        mine = pl.ds(32 * me, 32)
        dg[k, mine, pl.ds(0, n)] = coupled.astype(jnp.bfloat16)

        def one(d, _):
            to = (me + d) % XY
            part = dg.at[k, mine, pl.ds(0, n)]
            copy(part, part, ag_s.at[k], ag_r.at[k], ga, xy_band(to)).start()
            return 0

        lax.fori_loop(1, XY, one, 0)

    def gather(k):
        n = GROUPS[k][1]
        arrived(dg.at[k, pl.ds(0, 480), pl.ds(0, n)], ag_r.at[k])

        def block(r, _):
            rows = pl.ds(256 * r, 256)
            dj[k, rows, pl.ds(0, n)] = (
                -lax.dot_general(
                    jm[...], dg[k, rows, pl.ds(0, n)], NN, preferred_element_type=jnp.float32
                )
            ).astype(jnp.bfloat16)
            return 0

        lax.fori_loop(0, 2, block, 0)

    def second_piece(i, g, q, groups, first, last):
        def block(r, _):
            rows = pl.ds(pl.multiple_of(256 * r, 256), 256)
            total = None
            for k in groups:
                start, n = GROUPS[k]
                re = lax.dot_general(
                    dg[k, rows, pl.ds(0, n)], pc[i, 0, pl.ds(start, n), :], NN,
                    preferred_element_type=jnp.float32,
                )
                im = lax.dot_general(
                    dj[k, rows, pl.ds(0, n)], pc[i, 1, pl.ds(start, n), :], NN,
                    preferred_element_type=jnp.float32,
                )
                total = re + im if total is None else total + re + im
            if not first:
                total = total + acc[i, rows, :]
            if last:
                bands = pl.ds(pl.multiple_of(128 * r, 128), 128)
                ab[g, q, bands] = total.astype(jnp.bfloat16).reshape(128, 2, WIDTH)
            else:
                acc[i, rows, :] = total
            return 0

        lax.fori_loop(0, 2, block, 0)

    def second_product(groups, first):
        for i, g, q in pieces:
            second_piece(i, g, q, groups, first, False)

    for k in range(4):
        z_copy(k).wait_recv()
        fwd_copy(k).start()
        z_copy(k).wait_send()
        if k + 2 < 4:
            z_copy(k + 2).start()
        split(k, 1)
        fwd_copy(k).wait_recv()
        split(k, 3)
        first_product(k)
        rs_send(k)
        if k >= 1:
            z_sum(k - 1)
        if k >= 2:
            couple(k - 2)
    couple(2)
    gather(0)
    z_sum(3)
    gather(1)
    second_product((0, 1), True)
    couple(3)
    gather(2)
    second_product((2,), False)
    gather(3)

    def back_copy(k, c, q):
        return copy(
            ab.at[c, q, pl.ds(16 * k, 16)],
            out.at[pl.ds(16 * core, 16), :, columns(me, q)],
            b_s, b_r.at[core], zl * NC + c, xy_band(k),
        )

    for side, c in ((2, 1 - core), (0, core)):
        for i, g, q in pieces[side : side + 1] + pieces[side + 1 : side + 2]:
            second_piece(i, g, q, (3,), False, True)

        def back_send(d, _):
            k = (me + d) % XY
            for q in range(NH):
                back_copy(k, c, q).start()
            return 0

        lax.fori_loop(1, XY, back_send, 0)
        if side == 2:
            for q in range(NH):
                back_copy(me, c, q).start()
    local = [
        pltpu.make_async_copy(
            ab.at[core, q, pl.ds(16 * me, 16)],
            out.at[pl.ds(16 * core, 16), :, columns(me, q)],
            loc_s.at[q],
        )
        for q in range(NH)
    ]
    for q in range(NH):
        local[q].start()

    for k in range(4):
        n = GROUPS[k][1]
        core_copy(k).wait_send()
        fwd_copy(k).wait_send()
        left(rb.at[k, :, :, pl.ds(0, n)], rs_s.at[k])
        left(zr.at[k, :, :, pl.ds(0, n)], z_s.at[k])
        left(dg.at[k, pl.ds(0, 480), pl.ds(0, n)], ag_s.at[k])
    left(xr.at[0], o_s)
    left(xr.at[0, :, pl.ds(0, 240)], o_s)
    left(ab.at[0], b_s)
    left(ab.at[0, :, pl.ds(0, 240)], b_s)
    for q in range(NH):
        local[q].wait()
    arrived(ab.at[core, :, pl.ds(0, 240)], b_r.at[core])
    arrived(ab.at[1 - core], b_r.at[1 - core])


def per_device(orbitals, projectors, coupling, species, offsets):
    bf16, f32 = jnp.bfloat16, jnp.float32
    vmem = pl.BlockSpec(memory_space=pltpu.VMEM)
    hbm = pl.BlockSpec(memory_space=pltpu.HBM)
    dma = pltpu.SemaphoreType.DMA
    return pl.pallas_call(
        kernel,
        out_shape=jax.ShapeDtypeStruct(orbitals.shape, bf16),
        in_specs=[hbm, hbm, vmem, vmem, vmem],
        out_specs=hbm,
        scratch_shapes=[
            pltpu.VMEM((4, ROWS, 2, WIDTH), bf16),
            pltpu.VMEM((4, 2, ROWS, WIDTH), bf16),
            pltpu.VMEM((2, 2, 256, 2, WIDTH), bf16),
            pltpu.VMEM((2, 2, 512, WIDTH), bf16),
            pltpu.VMEM((2, 2, 512, WIDTH), bf16),
            pltpu.VMEM((256, 256), bf16),
            pltpu.VMEM((256, 256), bf16),
            pltpu.VMEM((4, 256, 256), f32),
            pltpu.VMEM((128, 128), f32),
            pltpu.VMEM((4, 512, 256), bf16),
            pltpu.VMEM((4, XY - 1, 32, 256), bf16),
            pltpu.VMEM((4, 32, 256), f32),
            pltpu.VMEM((4, 32, 256), bf16),
            pltpu.VMEM((4, NZ - 1, 32, 256), bf16),
            pltpu.VMEM((4, 512, 256), bf16),
            pltpu.VMEM((4, 512, 256), bf16),
            pltpu.VMEM((4, 512, WIDTH), f32),
            pltpu.VMEM((2, 2, 256, 2, WIDTH), bf16),
            dma((4,)), dma((4,)), dma((4,)), dma((4,)), dma((4,)), dma((4,)),
            dma, dma((2,)), dma((4,)), dma((4,)), dma((4,)), dma((4,)),
            dma((4,)), dma((4,)), dma, dma((2,)), dma((4,)), dma((2,)), dma((2,)),
        ],
        compiler_params=pltpu.CompilerParams(collective_id=0, has_side_effects=True),
    )(
        orbitals, projectors, coupling.transpose(1, 0, 2),
        species.reshape(1, -1), offsets.reshape(1, -1),
    )


def solution(mesh):
    placed = (P("band", None, "ga"), P(None, None, ("ga", "band")), P(), P(), P())
    return jax.shard_map(
        per_device, mesh=mesh, in_specs=placed, out_specs=P("band", None, "ga"), check_vma=False
    )
```

time: 110 us -> 94.9 us (0.86)
  the two profiles are of different devices: /device:TPU:57 before, /device:TPU:32 now
where the time goes in v2:
time: 94.9 us; the launch traced here: 94.6 us
  Pallas kernels  91.2 us (96%)
  local copies, waits for them, and re-layouts  3.45 us (4%)
    pallas_call x1, Pallas kernels, per_device(): pl.pallas_call(kernel, out_shape=jax.ShapeDtypeStruct(orbitals.shape, bf1...  91.2 us
    unnamed x1, local copies, waits for them, and re-layouts  3.45 us

profile of v2, /device:TPU:32, one launch (start us, length us, event | category | flops | bytes accessed | tf_op | source)
XLA Modules:
  0.0 94.6 jit_solution(6360876229715247885)
XLA Ops:
  0.0 91.2 %shard_map.55 = bf16[32,2,8192]{2,1,0:T(2,128)(2,1)} custom-call(bf16[32,2,8192]{2,1,0:T(2,128)(2,1)} %orb.1, bf16[864,2,256]{2,1,0:T(2,128)(2,1)} %proj.1, f32[18,4,18]{2,1,0:T(4,128)} %bitcast.3, s32[1,48]{1,0:T(1,128)} %bitcast.4, s32[1,48]{1,0:T(1,128)} %bitcast.5), custom_call_target="tpu_custom_call" | custom-call | tf_op jit(solution)/shard_map/pallas_call | solution.py:423
  91.2 3.4 %copy.7 = bf16[32,2,8192]{2,1,0:T(2,128)(2,1)} copy(bf16[32,2,8192]{2,1,0:T(2,128)(2,1)} %shard_map.55) | data formatting | bytes 2097152

commit v3 on v2

--- a/solution.py
+++ b/solution.py
@@ -60,10 +60,11 @@
 
 
 def kernel(
-    orb, proj, coup, species, offsets, out,
+    orb, proj, coup_hbm, species_hbm, offsets_hbm, out,
     praw, pc, xr, xt, xj, jm, pm, cm, cpad, sb, rb, town, zs, zr, dg, dj, acc, ab,
     pz_s, pz_r, pd_s, pd_r, pf_s, pf_r, o_s, o_r, rs_s, rs_r, z_s, z_r, ag_s, ag_r, b_s, b_r,
-    own_s, oo_s, loc_s,
+    own_s, oo_s,
+    coup, species, offsets, small_s, pacc,
 ):
     ga = lax.axis_index("ga")
     band = lax.axis_index("band")
@@ -143,8 +144,8 @@
             )
 
     pl.semaphore_wait(barrier, 1 + (NZ - 1) + 1 + 2 * (XY - 1))
-    z_copy(0).start()
-    z_copy(1).start()
+    for k in range(4):
+        z_copy(k).start()
 
     def orb_copy(k, c, q):
         return copy(
@@ -174,10 +175,19 @@
         own_orb[q].start()
     for k in range(4):
         core_copy(k).start()
+    small = [
+        pltpu.make_async_copy(coup_hbm, coup, small_s.at[0]),
+        pltpu.make_async_copy(species_hbm, species, small_s.at[1]),
+        pltpu.make_async_copy(offsets_hbm, offsets, small_s.at[2]),
+    ]
+    for one in small:
+        one.start()
 
     jm[...] = turn_matrix()
     pm[...] = split_matrix()
     cpad[...] = jnp.zeros_like(cpad)
+    for one in small:
+        one.wait()
     for i in range(PER_ATOM):
         cpad[pl.ds(4 * i, 4), pl.ds(0, PER_ATOM)] = coup[i]
     for k in range(4):
@@ -225,23 +235,38 @@
 
     pieces = ((0, core, h), (1, core, 1 - h), (2, 1 - core, h), (3, 1 - core, 1 - h))
 
+    def pieces_product(k, r, chosen):
+        start, n = GROUPS[k]
+        rows = pl.ds(pl.multiple_of(256 * r, 256), 256)
+        total = None
+        for i, g, q in chosen:
+            re = lax.dot_general(
+                xt[g, q, rows, :], pc[i, 0, pl.ds(start, n), :], NT,
+                preferred_element_type=jnp.float32,
+            )
+            im = lax.dot_general(
+                xj[g, q, rows, :], pc[i, 1, pl.ds(start, n), :], NT,
+                preferred_element_type=jnp.float32,
+            )
+            total = re + im if total is None else total + re + im
+        return rows, total
+
+    def first_early(k):
+        n = GROUPS[k][1]
+
+        def block(r, _):
+            rows, total = pieces_product(k, r, (pieces[0], pieces[2]))
+            pacc[rows, pl.ds(0, n)] = total
+            return 0
+
+        lax.fori_loop(0, 2, block, 0)
+
     def first_product(k):
-        start, n = GROUPS[k]
+        n = GROUPS[k][1]
 
         def block(r, _):
-            rows = pl.ds(256 * r, 256)
-            total = None
-            for i, g, q in pieces:
-                re = lax.dot_general(
-                    xt[g, q, rows, :], pc[i, 0, pl.ds(start, n), :], NT,
-                    preferred_element_type=jnp.float32,
-                )
-                im = lax.dot_general(
-                    xj[g, q, rows, :], pc[i, 1, pl.ds(start, n), :], NT,
-                    preferred_element_type=jnp.float32,
-                )
-                total = re + im if total is None else total + re + im
-            sb[k, rows, pl.ds(0, n)] = total.astype(jnp.bfloat16)
+            rows, total = pieces_product(k, r, (pieces[1], pieces[3]))
+            sb[k, rows, pl.ds(0, n)] = (total + pacc[rows, pl.ds(0, n)]).astype(jnp.bfloat16)
             return 0
 
         lax.fori_loop(0, 2, block, 0)
@@ -342,11 +367,9 @@
             second_piece(i, g, q, groups, first, False)
 
     for k in range(4):
+        first_early(k)
         z_copy(k).wait_recv()
         fwd_copy(k).start()
-        z_copy(k).wait_send()
-        if k + 2 < 4:
-            z_copy(k + 2).start()
         split(k, 1)
         fwd_copy(k).wait_recv()
         split(k, 3)
@@ -387,19 +410,12 @@
         if side == 2:
             for q in range(NH):
                 back_copy(me, c, q).start()
-    local = [
-        pltpu.make_async_copy(
-            ab.at[core, q, pl.ds(16 * me, 16)],
-            out.at[pl.ds(16 * core, 16), :, columns(me, q)],
-            loc_s.at[q],
-        )
-        for q in range(NH)
-    ]
     for q in range(NH):
-        local[q].start()
-
-    for k in range(4):
-        n = GROUPS[k][1]
+        out[pl.ds(16 * core, 16), :, columns(me, q)] = ab[core, q, pl.ds(16 * me, 16)]
+
+    for k in range(4):
+        n = GROUPS[k][1]
+        z_copy(k).wait_send()
         core_copy(k).wait_send()
         fwd_copy(k).wait_send()
         left(rb.at[k, :, :, pl.ds(0, n)], rs_s.at[k])
@@ -409,8 +425,6 @@
     left(xr.at[0, :, pl.ds(0, 240)], o_s)
     left(ab.at[0], b_s)
     left(ab.at[0, :, pl.ds(0, 240)], b_s)
-    for q in range(NH):
-        local[q].wait()
     arrived(ab.at[core, :, pl.ds(0, 240)], b_r.at[core])
     arrived(ab.at[1 - core], b_r.at[1 - core])
 
@@ -422,9 +436,9 @@
     dma = pltpu.SemaphoreType.DMA
     return pl.pallas_call(
         kernel,
-        out_shape=jax.ShapeDtypeStruct(orbitals.shape, bf16),
-        in_specs=[hbm, hbm, vmem, vmem, vmem],
-        out_specs=hbm,
+        out_shape=pltpu.VMEM(orbitals.shape, bf16),
+        in_specs=[hbm] * 5,
+        out_specs=vmem,
         scratch_shapes=[
             pltpu.VMEM((4, ROWS, 2, WIDTH), bf16),
             pltpu.VMEM((4, 2, ROWS, WIDTH), bf16),
@@ -446,7 +460,12 @@
             pltpu.VMEM((2, 2, 256, 2, WIDTH), bf16),
             dma((4,)), dma((4,)), dma((4,)), dma((4,)), dma((4,)), dma((4,)),
             dma, dma((2,)), dma((4,)), dma((4,)), dma((4,)), dma((4,)),
-            dma((4,)), dma((4,)), dma, dma((2,)), dma((4,)), dma((2,)), dma((2,)),
+            dma((4,)), dma((4,)), dma, dma((2,)), dma((4,)), dma((2,)),
+            pltpu.VMEM((PER_ATOM, 4, PER_ATOM), f32),
+            pltpu.VMEM((1, 48), jnp.int32),
+            pltpu.VMEM((1, 48), jnp.int32),
+            dma((3,)),
+            pltpu.VMEM((512, 256), f32),
         ],
         compiler_params=pltpu.CompilerParams(collective_id=0, has_side_effects=True),
     )(

time: 94.9 us -> 91.6 us (0.965)
  local copies, waits for them, and re-layouts: 3.45 us -> 0.97 us
    unnamed x1, local copies, waits for them, and re-layouts: 3.45 us -> 0.97 us
where the time goes in v3:
time: 91.6 us; the launch traced here: 91.4 us
  Pallas kernels  90.5 us (99%)
  local copies, waits for them, and re-layouts  0.97 us (1%)
    pallas_call x1, Pallas kernels, per_device(): pl.pallas_call(kernel, out_shape=pltpu.VMEM(orbitals.shape, bf16), in_spe...  90.5 us

profile of v3, /device:TPU:32, one launch (start us, length us, event | category | flops | bytes accessed | tf_op | source)
XLA Modules:
  0.0 91.4 jit_solution(8685713165902347983)
XLA Ops:
  0.0 90.5 %shard_map.55 = bf16[32,2,8192]{2,1,0:T(2,128)(2,1)S(1)} custom-call(bf16[32,2,8192]{2,1,0:T(2,128)(2,1)} %orb.1, bf16[864,2,256]{2,1,0:T(2,128)(2,1)} %proj.1, f32[18,4,18]{2,1,0:T(4,128)} %bitcast.3, s32[1,48]{1,0:T(1,128)} %bitcast.4, s32[1,48]{1,0:T(1,128)} %bitcast.5), custom_call_target="tpu_custom_call" | custom-call | tf_op jit(solution)/shard_map/pallas_call | solution.py:437
  90.5 1.0 %copy.7 = bf16[32,2,8192]{2,1,0:T(2,128)(2,1)} copy(bf16[32,2,8192]{2,1,0:T(2,128)(2,1)S(1)} %shard_map.55) | data formatting | bytes 2097152

commit v4 on v3

--- a/solution.py
+++ b/solution.py
@@ -13,6 +13,11 @@
 WIDTH = 256
 ROWS = 896
 COUNTS = (252, 252, 252, 108)
+OFFSETS = sorted(
+    ((dx, dy) for dx in range(NX) for dy in range(NY)),
+    key=lambda at: (min(at[0], NX - at[0]) + min(at[1], NY - at[1]), at),
+)
+BATCHES = ((0, 5), (5, 11), (11, 16))
 HIGHEST = lax.Precision.HIGHEST
 NT = (((1,), (1,)), ((), ()))
 NN = (((1,), (0,)), ((), ()))
@@ -72,6 +77,10 @@
     x, h, y = band // (NH * NY), band // NY % NH, band % NY
     me = x * NY + y
 
+    def apart(offset, sign):
+        dx, dy = offset
+        return (x + NX + sign * dx) % NX * (NH * NY) + h * NY + (y + NY + sign * dy) % NY
+
     def xy_band(k):
         return k // NY * (NH * NY) + h * NY + k % NY
 
@@ -310,20 +319,25 @@
             total, cm[k, pl.ds(0, n), pl.ds(0, n)], NT, precision=HIGHEST,
             preferred_element_type=jnp.float32,
         )
-        mine = pl.ds(32 * me, 32)
-        dg[k, mine, pl.ds(0, n)] = coupled.astype(jnp.bfloat16)
-
-        def one(d, _):
-            to = (me + d) % XY
-            part = dg.at[k, mine, pl.ds(0, n)]
-            copy(part, part, ag_s.at[k], ag_r.at[k], ga, xy_band(to)).start()
-            return 0
-
-        lax.fori_loop(1, XY, one, 0)
+        dg[k, pl.ds(0, 32), pl.ds(0, n)] = coupled.astype(jnp.bfloat16)
+        for batch, (first, end) in enumerate(BATCHES):
+            for slot in range(max(first, 1), end):
+                copy(
+                    dg.at[k, pl.ds(0, 32), pl.ds(0, n)],
+                    dg.at[k, pl.ds(32 * slot, 32), pl.ds(0, n)],
+                    ag_s.at[k], ag_r.at[k, batch], ga, apart(OFFSETS[slot], -1),
+                ).start()
+
+    def gather_batch(k, batch):
+        first, end = BATCHES[batch]
+        first = max(first, 1)
+        n = GROUPS[k][1]
+        arrived(dg.at[k, pl.ds(32 * first, 32 * (end - first)), pl.ds(0, n)], ag_r.at[k, batch])
 
     def gather(k):
         n = GROUPS[k][1]
-        arrived(dg.at[k, pl.ds(0, 480), pl.ds(0, n)], ag_r.at[k])
+        for batch in range(3):
+            gather_batch(k, batch)
 
         def block(r, _):
             rows = pl.ds(256 * r, 256)
@@ -336,7 +350,7 @@
 
         lax.fori_loop(0, 2, block, 0)
 
-    def second_piece(i, g, q, groups, first, last):
+    def second_piece(i, groups, first):
         def block(r, _):
             rows = pl.ds(pl.multiple_of(256 * r, 256), 256)
             total = None
@@ -353,18 +367,14 @@
                 total = re + im if total is None else total + re + im
             if not first:
                 total = total + acc[i, rows, :]
-            if last:
-                bands = pl.ds(pl.multiple_of(128 * r, 128), 128)
-                ab[g, q, bands] = total.astype(jnp.bfloat16).reshape(128, 2, WIDTH)
-            else:
-                acc[i, rows, :] = total
+            acc[i, rows, :] = total
             return 0
 
         lax.fori_loop(0, 2, block, 0)
 
     def second_product(groups, first):
-        for i, g, q in pieces:
-            second_piece(i, g, q, groups, first, False)
+        for i in range(4):
+            second_piece(i, groups, first)
 
     for k in range(4):
         first_early(k)
@@ -387,31 +397,43 @@
     couple(3)
     gather(2)
     second_product((2,), False)
-    gather(3)
-
-    def back_copy(k, c, q):
+
+    def back_copy(slot, c, q):
         return copy(
-            ab.at[c, q, pl.ds(16 * k, 16)],
+            ab.at[c, q, pl.ds(16 * slot, 16)],
             out.at[pl.ds(16 * core, 16), :, columns(me, q)],
-            b_s, b_r.at[core], zl * NC + c, xy_band(k),
-        )
-
-    for side, c in ((2, 1 - core), (0, core)):
-        for i, g, q in pieces[side : side + 1] + pieces[side + 1 : side + 2]:
-            second_piece(i, g, q, (3,), False, True)
-
-        def back_send(d, _):
-            k = (me + d) % XY
-            for q in range(NH):
-                back_copy(k, c, q).start()
-            return 0
-
-        lax.fori_loop(1, XY, back_send, 0)
-        if side == 2:
-            for q in range(NH):
-                back_copy(me, c, q).start()
+            b_s, b_r.at[core], zl * NC + c, apart(OFFSETS[slot], 1),
+        )
+
+    start, n = GROUPS[3]
+    for batch, (first, end) in enumerate(BATCHES):
+        gather_batch(3, batch)
+        rows = pl.ds(32 * first, 32 * (end - first))
+        value = dg[3, rows, pl.ds(0, n)].astype(jnp.float32)
+        height = value.shape[0]
+        even = (lax.broadcasted_iota(jnp.int32, value.shape, 0) & 1) == 0
+        turned = jnp.where(
+            even, -pltpu.roll(value, height - 1, 0), pltpu.roll(value, 1, 0)
+        ).astype(jnp.bfloat16)
+        for side, c in ((2, 1 - core), (0, core)):
+            for i, g, q in pieces[side : side + 2]:
+                re = lax.dot_general(
+                    dg[3, rows, pl.ds(0, n)], pc[i, 0, pl.ds(start, n), :], NN,
+                    preferred_element_type=jnp.float32,
+                )
+                im = lax.dot_general(
+                    turned, pc[i, 1, pl.ds(start, n), :], NN,
+                    preferred_element_type=jnp.float32,
+                )
+                ab[g, q, pl.ds(16 * first, 16 * (end - first))] = (
+                    (re + im + acc[i, rows, :]).astype(jnp.bfloat16).reshape(height // 2, 2, WIDTH)
+                )
+            for slot in range(first, end):
+                for q in range(NH):
+                    if slot > 0 or side == 2:
+                        back_copy(slot, c, q).start()
     for q in range(NH):
-        out[pl.ds(16 * core, 16), :, columns(me, q)] = ab[core, q, pl.ds(16 * me, 16)]
+        out[pl.ds(16 * core, 16), :, columns(me, q)] = ab[core, q, pl.ds(0, 16)]
 
     for k in range(4):
         n = GROUPS[k][1]
@@ -460,7 +482,7 @@
             pltpu.VMEM((2, 2, 256, 2, WIDTH), bf16),
             dma((4,)), dma((4,)), dma((4,)), dma((4,)), dma((4,)), dma((4,)),
             dma, dma((2,)), dma((4,)), dma((4,)), dma((4,)), dma((4,)),
-            dma((4,)), dma((4,)), dma, dma((2,)), dma((4,)), dma((2,)),
+            dma((4,)), dma((4, 3)), dma, dma((2,)), dma((4,)), dma((2,)),
             pltpu.VMEM((PER_ATOM, 4, PER_ATOM), f32),
             pltpu.VMEM((1, 48), jnp.int32),
             pltpu.VMEM((1, 48), jnp.int32),

time: 91.6 us -> 89.1 us (0.973)
  Pallas kernels: 90.5 us -> 88 us
    pallas_call x1, Pallas kernels: 90.5 us -> 88 us  [per_device(): pl.pallas_call(kernel, out_shape=pltpu.VMEM(orbitals.shape, bf16), in_spe...]
where the time goes in v4:
time: 89.1 us; the launch traced here: 88.9 us
  Pallas kernels  88 us (99%)
  local copies, waits for them, and re-layouts  0.97 us (1%)
    pallas_call x1, Pallas kernels, per_device(): pl.pallas_call(kernel, out_shape=pltpu.VMEM(orbitals.shape, bf16), in_spe...  88 us

profile of v4, /device:TPU:32, one launch (start us, length us, event | category | flops | bytes accessed | tf_op | source)
XLA Modules:
  0.0 88.9 jit_solution(12446735823069971922)
XLA Ops:
  0.0 88.0 %shard_map.55 = bf16[32,2,8192]{2,1,0:T(2,128)(2,1)S(1)} custom-call(bf16[32,2,8192]{2,1,0:T(2,128)(2,1)} %orb.1, bf16[864,2,256]{2,1,0:T(2,128)(2,1)} %proj.1, f32[18,4,18]{2,1,0:T(4,128)} %bitcast.3, s32[1,48]{1,0:T(1,128)} %bitcast.4, s32[1,48]{1,0:T(1,128)} %bitcast.5), custom_call_target="tpu_custom_call" | custom-call | tf_op jit(solution)/shard_map/pallas_call | solution.py:459
  88.0 1.0 %copy.7 = bf16[32,2,8192]{2,1,0:T(2,128)(2,1)} copy(bf16[32,2,8192]{2,1,0:T(2,128)(2,1)S(1)} %shard_map.55) | data formatting | bytes 2097152

commit v5 on v4

--- a/solution.py
+++ b/solution.py
@@ -8,11 +8,12 @@
 NX, NY, NH, NZ, NC = 4, 4, 2, 4, 2
 XY = NX * NY
 PER_ATOM = 18
-GROUP_ATOMS = 14
-GROUPS = ((0, 256), (256, 256), (512, 256), (768, 128))
+FIRST_ATOM = (0, 21, 35, 42)
+GROUPS = ((0, 384), (384, 256), (640, 128), (768, 128))
+WIDEST = 384
 WIDTH = 256
 ROWS = 896
-COUNTS = (252, 252, 252, 108)
+COUNTS = (378, 252, 126, 108)
 OFFSETS = sorted(
     ((dx, dy) for dx in range(NX) for dy in range(NY)),
     key=lambda at: (min(at[0], NX - at[0]) + min(at[1], NY - at[1]), at),
@@ -24,27 +25,28 @@
 
 
 def coupling_matrix(group, cpad, species, offsets):
-    row = lax.broadcasted_iota(jnp.int32, (256, 1), 0)
+    n = GROUPS[group][1]
+    row = lax.broadcasted_iota(jnp.int32, (n, 1), 0)
     row_atom = (row * 3641) >> 16
     row_in = row - row_atom * PER_ATOM
-    start = (row_atom + GROUP_ATOMS * group) * PER_ATOM
+    start = (row_atom + FIRST_ATOM[group]) * PER_ATOM
     kind = jnp.sum(
         jnp.where(offsets == start, species.astype(jnp.float32), 0.0), axis=1, keepdims=True
     )
-    col = lax.broadcasted_iota(jnp.int32, (256, 128), 1)
+    col = lax.broadcasted_iota(jnp.int32, (n, 128), 1)
     col_in, col_kind = col >> 2, col & 3
     pick = jnp.where(
         (col_kind.astype(jnp.float32) == kind) & (col_in == row_in), 1.0, 0.0
     ).astype(jnp.float32)
     rows = lax.dot_general(pick, cpad, NN, precision=HIGHEST, preferred_element_type=jnp.float32)
-    wide = lax.broadcasted_iota(jnp.int32, (128, 256), 1)
+    wide = lax.broadcasted_iota(jnp.int32, (128, n), 1)
     wide_atom = (wide * 3641) >> 16
     spread = jnp.where(
-        wide - wide_atom * PER_ATOM == lax.broadcasted_iota(jnp.int32, (128, 256), 0), 1.0, 0.0
+        wide - wide_atom * PER_ATOM == lax.broadcasted_iota(jnp.int32, (128, n), 0), 1.0, 0.0
     ).astype(jnp.float32)
     full = lax.dot_general(rows, spread, NN, precision=HIGHEST, preferred_element_type=jnp.float32)
-    full_row = lax.broadcasted_iota(jnp.int32, (256, 256), 0)
-    full_col = lax.broadcasted_iota(jnp.int32, (256, 256), 1)
+    full_row = lax.broadcasted_iota(jnp.int32, (n, n), 0)
+    full_col = lax.broadcasted_iota(jnp.int32, (n, n), 1)
     same = ((full_row * 3641) >> 16) == ((full_col * 3641) >> 16)
     return jnp.where(same, full, 0.0)
 
@@ -106,7 +108,7 @@
         return pl.ds(GROUPS[k][0], COUNTS[k])
 
     def source(k):
-        return proj.at[pl.ds(GROUP_ATOMS * PER_ATOM * k, COUNTS[k])]
+        return proj.at[pl.ds(PER_ATOM * FIRST_ATOM[k], COUNTS[k])]
 
     def columns(k, q):
         block = k // NY * (NH * NY) + q * NY + k % NY
@@ -200,7 +202,10 @@
     for i in range(PER_ATOM):
         cpad[pl.ds(4 * i, 4), pl.ds(0, PER_ATOM)] = coup[i]
     for k in range(4):
-        cm[k] = coupling_matrix(k, cpad[...], species[...], offsets[...])
+        n = GROUPS[k][1]
+        cm[k, pl.ds(0, n), pl.ds(0, n)] = coupling_matrix(
+            k, cpad[...], species[...], offsets[...]
+        )
 
     for k in range(4):
         own[k].wait()
@@ -469,15 +474,15 @@
             pltpu.VMEM((2, 2, 512, WIDTH), bf16),
             pltpu.VMEM((256, 256), bf16),
             pltpu.VMEM((256, 256), bf16),
-            pltpu.VMEM((4, 256, 256), f32),
+            pltpu.VMEM((4, WIDEST, WIDEST), f32),
             pltpu.VMEM((128, 128), f32),
-            pltpu.VMEM((4, 512, 256), bf16),
-            pltpu.VMEM((4, XY - 1, 32, 256), bf16),
-            pltpu.VMEM((4, 32, 256), f32),
-            pltpu.VMEM((4, 32, 256), bf16),
-            pltpu.VMEM((4, NZ - 1, 32, 256), bf16),
-            pltpu.VMEM((4, 512, 256), bf16),
-            pltpu.VMEM((4, 512, 256), bf16),
+            pltpu.VMEM((4, 512, WIDEST), bf16),
+            pltpu.VMEM((4, XY - 1, 32, WIDEST), bf16),
+            pltpu.VMEM((4, 32, WIDEST), f32),
+            pltpu.VMEM((4, 32, WIDEST), bf16),
+            pltpu.VMEM((4, NZ - 1, 32, WIDEST), bf16),
+            pltpu.VMEM((4, 512, WIDEST), bf16),
+            pltpu.VMEM((4, 512, WIDEST), bf16),
             pltpu.VMEM((4, 512, WIDTH), f32),
             pltpu.VMEM((2, 2, 256, 2, WIDTH), bf16),
             dma((4,)), dma((4,)), dma((4,)), dma((4,)), dma((4,)), dma((4,)),
@@ -487,7 +492,7 @@
             pltpu.VMEM((1, 48), jnp.int32),
             pltpu.VMEM((1, 48), jnp.int32),
             dma((3,)),
-            pltpu.VMEM((512, 256), f32),
+            pltpu.VMEM((512, WIDEST), f32),
         ],
         compiler_params=pltpu.CompilerParams(collective_id=0, has_side_effects=True),
     )(

time: 89.1 us -> 91.3 us (1.025)
  Pallas kernels: 88 us -> 89.3 us
    pallas_call x1, Pallas kernels: 88 us -> 89.3 us  [per_device(): pl.pallas_call(kernel, out_shape=pltpu.VMEM(orbitals.shape, bf16), in_spe...]
where the time goes in v5:
time: 91.3 us; the launch traced here: 90.2 us
  Pallas kernels  89.3 us (98%)
  local copies, waits for them, and re-layouts  0.97 us (1%)
    pallas_call x1, Pallas kernels, per_device(): pl.pallas_call(kernel, out_shape=pltpu.VMEM(orbitals.shape, bf16), in_spe...  89.3 us

profile of v5, /device:TPU:32, one launch (start us, length us, event | category | flops | bytes accessed | tf_op | source)
XLA Modules:
  0.0 90.2 jit_solution(16116859577938594098)
XLA Ops:
  0.0 89.3 %shard_map.55 = bf16[32,2,8192]{2,1,0:T(2,128)(2,1)S(1)} custom-call(bf16[32,2,8192]{2,1,0:T(2,128)(2,1)} %orb.1, bf16[864,2,256]{2,1,0:T(2,128)(2,1)} %proj.1, f32[18,4,18]{2,1,0:T(4,128)} %bitcast.3, s32[1,48]{1,0:T(1,128)} %bitcast.4, s32[1,48]{1,0:T(1,128)} %bitcast.5), custom_call_target="tpu_custom_call" | custom-call | tf_op jit(solution)/shard_map/pallas_call | solution.py:464
  89.3 1.0 %copy.7 = bf16[32,2,8192]{2,1,0:T(2,128)(2,1)} copy(bf16[32,2,8192]{2,1,0:T(2,128)(2,1)S(1)} %shard_map.55) | data formatting | bytes 2097152

commit v6 on v4

--- a/solution.py
+++ b/solution.py
@@ -385,15 +385,18 @@
         split(k, 3)
         first_product(k)
         rs_send(k)
-        if k >= 1:
-            z_sum(k - 1)
-        if k >= 2:
-            couple(k - 2)
+        if k in (1, 2):
+            couple(k - 1)
+        if k in (0, 1):
+            z_sum(k)
+        if k == 2:
+            gather(0)
+    second_product((0,), True)
+    z_sum(2)
+    gather(1)
+    second_product((1,), False)
+    z_sum(3)
     couple(2)
-    gather(0)
-    z_sum(3)
-    gather(1)
-    second_product((0, 1), True)
     couple(3)
     gather(2)
     second_product((2,), False)

time: 89.1 us -> 97.2 us (1.091)
  the two profiles are of different devices: /device:TPU:32 before, /device:TPU:65 now
where the time goes in v6:
time: 97.2 us; the launch traced here: 97 us
  Pallas kernels  96 us (99%)
    pallas_call x1, Pallas kernels, per_device(): pl.pallas_call(kernel, out_shape=pltpu.VMEM(orbitals.shape, bf16), in_spe...  96 us

profile of v6, /device:TPU:65, one launch (start us, length us, event | category | flops | bytes accessed | tf_op | source)
XLA Modules:
  0.0 97.0 jit_solution(17675184743690329858)
XLA Ops:
  0.0 96.0 %shard_map.55 = bf16[32,2,8192]{2,1,0:T(2,128)(2,1)S(1)} custom-call(bf16[32,2,8192]{2,1,0:T(2,128)(2,1)} %orb.1, bf16[864,2,256]{2,1,0:T(2,128)(2,1)} %proj.1, f32[18,4,18]{2,1,0:T(4,128)} %bitcast.3, s32[1,48]{1,0:T(1,128)} %bitcast.4, s32[1,48]{1,0:T(1,128)} %bitcast.5), custom_call_target="tpu_custom_call" | custom-call | tf_op jit(solution)/shard_map/pallas_call | solution.py:462
  96.1 1.0 %copy.7 = bf16[32,2,8192]{2,1,0:T(2,128)(2,1)} copy(bf16[32,2,8192]{2,1,0:T(2,128)(2,1)S(1)} %shard_map.55) | data formatting | bytes 2097152

commit v7 on v4

--- a/solution.py
+++ b/solution.py
@@ -11,6 +11,7 @@
 GROUP_ATOMS = 14
 GROUPS = ((0, 256), (256, 256), (512, 256), (768, 128))
 WIDTH = 256
+LEVELS = 4
 ROWS = 896
 COUNTS = (252, 252, 252, 108)
 OFFSETS = sorted(
@@ -69,7 +70,7 @@
     praw, pc, xr, xt, xj, jm, pm, cm, cpad, sb, rb, town, zs, zr, dg, dj, acc, ab,
     pz_s, pz_r, pd_s, pd_r, pf_s, pf_r, o_s, o_r, rs_s, rs_r, z_s, z_r, ag_s, ag_r, b_s, b_r,
     own_s, oo_s,
-    coup, species, offsets, small_s, pacc,
+    coup, species, offsets, small_s, pacc, level_s,
 ):
     ga = lax.axis_index("ga")
     band = lax.axis_index("band")
@@ -112,24 +113,29 @@
         block = k // NY * (NH * NY) + q * NY + k % NY
         return pl.ds(pl.multiple_of(WIDTH * block, WIDTH), WIDTH)
 
-    def greet(to_ga, to_band):
+    def greet(sem, to_ga, to_band):
         pl.semaphore_signal(
-            barrier, inc=1, device_id={"ga": to_ga, "band": to_band},
+            sem, inc=1, device_id={"ga": to_ga, "band": to_band},
             device_id_type=pl.DeviceIdType.MESH,
         )
 
-    greet(ga, other_half)
-    for c in range(1, NZ):
-        greet((zl + c) % NZ * NC + core, band)
-    greet(other_core, band)
-
-    def greet_plane(d, _):
-        k = (me + d) % XY
-        greet(ga, xy_band(k))
-        greet(other_core, xy_band(k))
-        return 0
-
-    lax.fori_loop(1, XY, greet_plane, 0)
+    def greet_near(sem):
+        for offset in ((1, 0), (NX - 1, 0), (0, 1), (0, NY - 1)):
+            greet(sem, ga, apart(offset, 1))
+        greet(sem, other_core, band)
+
+        @pl.when(zl > 0)
+        def _():
+            greet(sem, ga - NC, band)
+
+        @pl.when(zl < NZ - 1)
+        def _():
+            greet(sem, ga + NC, band)
+
+    near = 5 + (zl + NZ - 1) // NZ + (2 * (NZ - 1) - 1 - zl) // (NZ - 1)
+    greet(barrier, ga, other_half)
+    greet_near(barrier)
+
     own = [pltpu.make_async_copy(source(k), praw.at[0, part(k)], own_s.at[k]) for k in range(4)]
     for k in range(4):
         own[k].start()
@@ -152,9 +158,14 @@
                 (pad, 2, WIDTH), jnp.bfloat16
             )
 
-    pl.semaphore_wait(barrier, 1 + (NZ - 1) + 1 + 2 * (XY - 1))
+    pl.semaphore_wait(barrier, near + 1)
     for k in range(4):
         z_copy(k).start()
+    for k in range(4):
+        core_copy(k).start()
+    for level in range(LEVELS):
+        greet_near(level_s.at[level])
+        pl.semaphore_wait(level_s.at[level], near)
 
     def orb_copy(k, c, q):
         return copy(
@@ -182,8 +193,6 @@
             )
         )
         own_orb[q].start()
-    for k in range(4):
-        core_copy(k).start()
     small = [
         pltpu.make_async_copy(coup_hbm, coup, small_s.at[0]),
         pltpu.make_async_copy(species_hbm, species, small_s.at[1]),
@@ -389,9 +398,9 @@
             z_sum(k - 1)
         if k >= 2:
             couple(k - 2)
-    couple(2)
     gather(0)
     z_sum(3)
+    couple(2)
     gather(1)
     second_product((0, 1), True)
     couple(3)
@@ -488,6 +497,7 @@
             pltpu.VMEM((1, 48), jnp.int32),
             dma((3,)),
             pltpu.VMEM((512, 256), f32),
+            pltpu.SemaphoreType.REGULAR((LEVELS,)),
         ],
         compiler_params=pltpu.CompilerParams(collective_id=0, has_side_effects=True),
     )(

time: 89.1 us -> 87.3 us (0.980)
  Pallas kernels: 88 us -> 86.2 us
    pallas_call x1, Pallas kernels: 88 us -> 86.2 us  [per_device(): pl.pallas_call(kernel, out_shape=pltpu.VMEM(orbitals.shape, bf16), in_spe...]
where the time goes in v7:
time: 87.3 us; the launch traced here: 87.2 us
  Pallas kernels  86.2 us (99%)
  local copies, waits for them, and re-layouts  0.97 us (1%)
    pallas_call x1, Pallas kernels, per_device(): pl.pallas_call(kernel, out_shape=pltpu.VMEM(orbitals.shape, bf16), in_spe...  86.2 us

profile of v7, /device:TPU:32, one launch (start us, length us, event | category | flops | bytes accessed | tf_op | source)
XLA Modules:
  0.0 87.2 jit_solution(2815133810382566688)
XLA Ops:
  0.0 86.2 %shard_map.55 = bf16[32,2,8192]{2,1,0:T(2,128)(2,1)S(1)} custom-call(bf16[32,2,8192]{2,1,0:T(2,128)(2,1)} %orb.1, bf16[864,2,256]{2,1,0:T(2,128)(2,1)} %proj.1, f32[18,4,18]{2,1,0:T(4,128)} %bitcast.3, s32[1,48]{1,0:T(1,128)} %bitcast.4, s32[1,48]{1,0:T(1,128)} %bitcast.5), custom_call_target="tpu_custom_call" | custom-call | tf_op jit(solution)/shard_map/pallas_call | solution.py:468
  86.2 1.0 %copy.7 = bf16[32,2,8192]{2,1,0:T(2,128)(2,1)} copy(bf16[32,2,8192]{2,1,0:T(2,128)(2,1)S(1)} %shard_map.55) | data formatting | bytes 2097152

commit v8 on v7

--- a/solution.py
+++ b/solution.py
@@ -18,7 +18,7 @@
     ((dx, dy) for dx in range(NX) for dy in range(NY)),
     key=lambda at: (min(at[0], NX - at[0]) + min(at[1], NY - at[1]), at),
 )
-BATCHES = ((0, 5), (5, 11), (11, 16))
+BATCHES = ((0, 5), (5, 8), (8, 16))
 HIGHEST = lax.Precision.HIGHEST
 NT = (((1,), (1,)), ((), ()))
 NN = (((1,), (0,)), ((), ()))
@@ -228,7 +228,7 @@
             pc[piece, 1, pl.ds(at, 128), :] = both[128:]
             return 0
 
-        lax.fori_loop(0, n // 128, block, 0)
+        lax.fori_loop(0, n // 128, block, 0, unroll=True)
 
     for k in range(4):
         split(k, 0)
@@ -277,7 +277,7 @@
             pacc[rows, pl.ds(0, n)] = total
             return 0
 
-        lax.fori_loop(0, 2, block, 0)
+        lax.fori_loop(0, 2, block, 0, unroll=True)
 
     def first_product(k):
         n = GROUPS[k][1]
@@ -287,7 +287,7 @@
             sb[k, rows, pl.ds(0, n)] = (total + pacc[rows, pl.ds(0, n)]).astype(jnp.bfloat16)
             return 0
 
-        lax.fori_loop(0, 2, block, 0)
+        lax.fori_loop(0, 2, block, 0, unroll=True)
 
     def rs_send(k):
         n = GROUPS[k][1]
@@ -301,7 +301,7 @@
             ).start()
             return 0
 
-        lax.fori_loop(1, XY, one, 0)
+        lax.fori_loop(1, XY, one, 0, unroll=True)
 
     def z_sum(k):
         n = GROUPS[k][1]
@@ -357,9 +357,9 @@
             ).astype(jnp.bfloat16)
             return 0
 
-        lax.fori_loop(0, 2, block, 0)
-
-    def second_piece(i, groups, first):
+        lax.fori_loop(0, 2, block, 0, unroll=True)
+
+    def second_piece(i, groups):
         def block(r, _):
             rows = pl.ds(pl.multiple_of(256 * r, 256), 256)
             total = None
@@ -374,16 +374,14 @@
                     preferred_element_type=jnp.float32,
                 )
                 total = re + im if total is None else total + re + im
-            if not first:
-                total = total + acc[i, rows, :]
             acc[i, rows, :] = total
             return 0
 
-        lax.fori_loop(0, 2, block, 0)
-
-    def second_product(groups, first):
+        lax.fori_loop(0, 2, block, 0, unroll=True)
+
+    def second_product(groups):
         for i in range(4):
-            second_piece(i, groups, first)
+            second_piece(i, groups)
 
     for k in range(4):
         first_early(k)
@@ -402,10 +400,8 @@
     z_sum(3)
     couple(2)
     gather(1)
-    second_product((0, 1), True)
+    second_product((0, 1))
     couple(3)
-    gather(2)
-    second_product((2,), False)
 
     def back_copy(slot, c, q):
         return copy(
@@ -414,28 +410,35 @@
             b_s, b_r.at[core], zl * NC + c, apart(OFFSETS[slot], 1),
         )
 
-    start, n = GROUPS[3]
+    late = (2, 3)
     for batch, (first, end) in enumerate(BATCHES):
-        gather_batch(3, batch)
         rows = pl.ds(32 * first, 32 * (end - first))
-        value = dg[3, rows, pl.ds(0, n)].astype(jnp.float32)
-        height = value.shape[0]
-        even = (lax.broadcasted_iota(jnp.int32, value.shape, 0) & 1) == 0
-        turned = jnp.where(
-            even, -pltpu.roll(value, height - 1, 0), pltpu.roll(value, 1, 0)
-        ).astype(jnp.bfloat16)
+        height = 32 * (end - first)
+        turned = {}
+        for k in late:
+            n = GROUPS[k][1]
+            gather_batch(k, batch)
+            value = dg[k, rows, pl.ds(0, n)].astype(jnp.float32)
+            even = (lax.broadcasted_iota(jnp.int32, value.shape, 0) & 1) == 0
+            turned[k] = jnp.where(
+                even, -pltpu.roll(value, height - 1, 0), pltpu.roll(value, 1, 0)
+            ).astype(jnp.bfloat16)
         for side, c in ((2, 1 - core), (0, core)):
             for i, g, q in pieces[side : side + 2]:
-                re = lax.dot_general(
-                    dg[3, rows, pl.ds(0, n)], pc[i, 0, pl.ds(start, n), :], NN,
-                    preferred_element_type=jnp.float32,
-                )
-                im = lax.dot_general(
-                    turned, pc[i, 1, pl.ds(start, n), :], NN,
-                    preferred_element_type=jnp.float32,
-                )
+                total = acc[i, rows, :]
+                for k in late:
+                    start, n = GROUPS[k]
+                    re = lax.dot_general(
+                        dg[k, rows, pl.ds(0, n)], pc[i, 0, pl.ds(start, n), :], NN,
+                        preferred_element_type=jnp.float32,
+                    )
+                    im = lax.dot_general(
+                        turned[k], pc[i, 1, pl.ds(start, n), :], NN,
+                        preferred_element_type=jnp.float32,
+                    )
+                    total = total + (re + im)
                 ab[g, q, pl.ds(16 * first, 16 * (end - first))] = (
-                    (re + im + acc[i, rows, :]).astype(jnp.bfloat16).reshape(height // 2, 2, WIDTH)
+                    total.astype(jnp.bfloat16).reshape(height // 2, 2, WIDTH)
                 )
             for slot in range(first, end):
                 for q in range(NH):

time: 87.3 us -> 85.2 us (0.976)
  Pallas kernels: 86.2 us -> 83.8 us
    pallas_call x1, Pallas kernels: 86.2 us -> 83.8 us  [per_device(): pl.pallas_call(kernel, out_shape=pltpu.VMEM(orbitals.shape, bf16), in_spe...]
where the time goes in v8:
time: 85.2 us; the launch traced here: 84.8 us
  Pallas kernels  83.8 us (98%)
  local copies, waits for them, and re-layouts  0.97 us (1%)
    pallas_call x1, Pallas kernels, per_device(): pl.pallas_call(kernel, out_shape=pltpu.VMEM(orbitals.shape, bf16), in_spe...  83.8 us

profile of v8, /device:TPU:32, one launch (start us, length us, event | category | flops | bytes accessed | tf_op | source)
XLA Modules:
  0.0 84.8 jit_solution(10805423656971779164)
XLA Ops:
  0.0 83.8 %shard_map.55 = bf16[32,2,8192]{2,1,0:T(2,128)(2,1)S(1)} custom-call(bf16[32,2,8192]{2,1,0:T(2,128)(2,1)} %orb.1, bf16[864,2,256]{2,1,0:T(2,128)(2,1)} %proj.1, f32[18,4,18]{2,1,0:T(4,128)} %bitcast.3, s32[1,48]{1,0:T(1,128)} %bitcast.4, s32[1,48]{1,0:T(1,128)} %bitcast.5), custom_call_target="tpu_custom_call" | custom-call | tf_op jit(solution)/shard_map/pallas_call | solution.py:471
  83.8 1.0 %copy.7 = bf16[32,2,8192]{2,1,0:T(2,128)(2,1)} copy(bf16[32,2,8192]{2,1,0:T(2,128)(2,1)S(1)} %shard_map.55) | data formatting | bytes 2097152

commit v9 on v8

--- a/solution.py
+++ b/solution.py
@@ -399,8 +399,7 @@
     gather(0)
     z_sum(3)
     couple(2)
-    gather(1)
-    second_product((0, 1))
+    second_product((0,))
     couple(3)
 
     def back_copy(slot, c, q):
@@ -410,7 +409,7 @@
             b_s, b_r.at[core], zl * NC + c, apart(OFFSETS[slot], 1),
         )
 
-    late = (2, 3)
+    late = (1, 2, 3)
     for batch, (first, end) in enumerate(BATCHES):
         rows = pl.ds(32 * first, 32 * (end - first))
         height = 32 * (end - first)

time: 85.2 us -> 84.9 us (level)
  no operation moved by 1% of the time
where the time goes in v9:
time: 84.9 us; the launch traced here: 84.2 us
  Pallas kernels  83.3 us (98%)
  local copies, waits for them, and re-layouts  0.97 us (1%)
    pallas_call x1, Pallas kernels, per_device(): pl.pallas_call(kernel, out_shape=pltpu.VMEM(orbitals.shape, bf16), in_spe...  83.3 us

profile of v9, /device:TPU:32, one launch (start us, length us, event | category | flops | bytes accessed | tf_op | source)
XLA Modules:
  0.0 84.2 jit_solution(10632587068831444748)
XLA Ops:
  0.0 83.3 %shard_map.55 = bf16[32,2,8192]{2,1,0:T(2,128)(2,1)S(1)} custom-call(bf16[32,2,8192]{2,1,0:T(2,128)(2,1)} %orb.1, bf16[864,2,256]{2,1,0:T(2,128)(2,1)} %proj.1, f32[18,4,18]{2,1,0:T(4,128)} %bitcast.3, s32[1,48]{1,0:T(1,128)} %bitcast.4, s32[1,48]{1,0:T(1,128)} %bitcast.5), custom_call_target="tpu_custom_call" | custom-call | tf_op jit(solution)/shard_map/pallas_call | solution.py:470
  83.3 1.0 %copy.7 = bf16[32,2,8192]{2,1,0:T(2,128)(2,1)} copy(bf16[32,2,8192]{2,1,0:T(2,128)(2,1)S(1)} %shard_map.55) | data formatting | bytes 2097152

commit v10 on v9

--- a/solution.py
+++ b/solution.py
@@ -279,11 +279,21 @@
 
         lax.fori_loop(0, 2, block, 0, unroll=True)
 
+    def first_arrived(k):
+        n = GROUPS[k][1]
+
+        def block(r, _):
+            rows, total = pieces_product(k, r, (pieces[1],))
+            pacc[rows, pl.ds(0, n)] = total + pacc[rows, pl.ds(0, n)]
+            return 0
+
+        lax.fori_loop(0, 2, block, 0, unroll=True)
+
     def first_product(k):
         n = GROUPS[k][1]
 
         def block(r, _):
-            rows, total = pieces_product(k, r, (pieces[1], pieces[3]))
+            rows, total = pieces_product(k, r, (pieces[3],))
             sb[k, rows, pl.ds(0, n)] = (total + pacc[rows, pl.ds(0, n)]).astype(jnp.bfloat16)
             return 0
 
@@ -388,6 +398,7 @@
         z_copy(k).wait_recv()
         fwd_copy(k).start()
         split(k, 1)
+        first_arrived(k)
         fwd_copy(k).wait_recv()
         split(k, 3)
         first_product(k)

time: 84.9 us -> 84.7 us (level)
  no operation moved by 1% of the time
where the time goes in v10:
time: 84.7 us; the launch traced here: 84.2 us
  Pallas kernels  83.2 us (98%)
  local copies, waits for them, and re-layouts  0.97 us (1%)
    pallas_call x1, Pallas kernels, per_device(): pl.pallas_call(kernel, out_shape=pltpu.VMEM(orbitals.shape, bf16), in_spe...  83.2 us

profile of v10, /device:TPU:32, one launch (start us, length us, event | category | flops | bytes accessed | tf_op | source)
XLA Modules:
  0.0 84.2 jit_solution(13483847200365308644)
XLA Ops:
  0.0 83.2 %shard_map.55 = bf16[32,2,8192]{2,1,0:T(2,128)(2,1)S(1)} custom-call(bf16[32,2,8192]{2,1,0:T(2,128)(2,1)} %orb.1, bf16[864,2,256]{2,1,0:T(2,128)(2,1)} %proj.1, f32[18,4,18]{2,1,0:T(4,128)} %bitcast.3, s32[1,48]{1,0:T(1,128)} %bitcast.4, s32[1,48]{1,0:T(1,128)} %bitcast.5), custom_call_target="tpu_custom_call" | custom-call | tf_op jit(solution)/shard_map/pallas_call | solution.py:481
  83.2 1.0 %copy.7 = bf16[32,2,8192]{2,1,0:T(2,128)(2,1)} copy(bf16[32,2,8192]{2,1,0:T(2,128)(2,1)S(1)} %shard_map.55) | data formatting | bytes 2097152
